TPU v7x, 32 devices: a whole 2x2x4 slice. The times are simulated.
32 devices in a mesh: dp: 2 (over x), ep: 16 (over z, y, core).
Axes of the slice: x: 2, y: 2, z: 4, core: 2. Of those that a mesh axis runs over, the one named last changes fastest.
Arguments:
- tok_in: bfloat16 [2048, 2048], P(('dp', 'ep')), parts along dimension 0
- lat_cache: bfloat16 [2048, 64, 512], P(('dp', 'ep')), parts along dimension 0
- rope_cache: bfloat16 [2048, 64, 64], P(('dp', 'ep')), parts along dimension 0
- tok_pos: int32 [2048], P(('dp', 'ep')), parts along dimension 0
- expert_ids: int32 [2048, 6], P(('dp', 'ep')), parts along dimension 0
- attn_gain: bfloat16 [2048], replicated
- w_query: bfloat16 [2048, 3072], replicated
- w_kvdown: bfloat16 [2048, 576], replicated
- w_ukey: bfloat16 [16, 128, 512], replicated
- w_uval: bfloat16 [16, 512, 128], replicated
- w_out: bfloat16 [2048, 2048], replicated
- ffn_gain: bfloat16 [2048], replicated
- w_router: bfloat16 [2048, 64], replicated
- sh_gate: bfloat16 [2048, 2816], replicated
- sh_up: bfloat16 [2048, 2816], replicated
- sh_down: bfloat16 [2816, 2048], replicated
- ex_gate: bfloat16 [64, 2048, 1408], P('ep')
- ex_up: bfloat16 [64, 2048, 1408], P('ep')
- ex_down: bfloat16 [64, 1408, 2048], P('ep')
Outputs:
- output 1: bfloat16 [2048, 2048], P(('dp', 'ep')), parts along dimension 0
- output 2: bfloat16 [2048, 64, 512], P(('dp', 'ep')), parts along dimension 0
- output 3: bfloat16 [2048, 64, 64], P(('dp', 'ep')), parts along dimension 0
There are 2 independent parts. A program takes and returns all parts, laid end to end along the dimension named above; an argument that names none is the same for every part.
All inputs are finite; a program needn't handle non-finite values.
Results may differ from a plain program's by a relative error of at most 0.013.
Values are sent between devices in bfloat16 or wider.
A program may use at most 1 GiB of HBM per device.

v0:
```python
import jax
import jax.numpy as jnp
from jax import lax
from jax.sharding import PartitionSpec as P

ROUTE_SCALE = 2.827
ROPE_BASE = 10000.0
NORM_EPS = 1e-6


def unit_norm(values):
    mean_sq = jnp.mean(jnp.square(values), axis=-1, keepdims=True)
    return values * lax.rsqrt(mean_sq + NORM_EPS)


def rms_norm(values, gain_vec):
    return unit_norm(values) * gain_vec.astype(jnp.float32)


def rope_rotate(values, angle_rad):
    half_dim = values.shape[-1] // 2
    x_first = values[..., :half_dim]
    x_second = values[..., half_dim:]
    cos_part = jnp.cos(angle_rad)
    sin_part = jnp.sin(angle_rad)
    return jnp.concatenate([x_first * cos_part - x_second * sin_part, x_second * cos_part + x_first * sin_part], axis=-1)


def attention_block(tok_in, lat_cache, rope_cache, tok_pos, attn_gain, w_query, w_kvdown, w_ukey, w_uval, w_out, ffn_gain):
    num_heads, nope_dim, kv_rank = w_ukey.shape
    rope_dim = rope_cache.shape[-1]
    seq_len = lat_cache.shape[1]
    tok_rows = tok_in.shape[0]
    x_wide = tok_in.astype(jnp.float32)
    x_norm = rms_norm(x_wide, attn_gain).astype(jnp.bfloat16)
    q_all = jnp.dot(x_norm, w_query, preferred_element_type=jnp.float32).astype(jnp.bfloat16).reshape(tok_rows, num_heads, nope_dim + rope_dim)
    kv_all = jnp.dot(x_norm, w_kvdown, preferred_element_type=jnp.float32)
    inv_freq = ROPE_BASE ** (-(2.0 * jnp.arange(rope_dim // 2)) / rope_dim)
    angle_rad = tok_pos.astype(jnp.float32)[:, None] * inv_freq[None, :]
    lat_new = unit_norm(kv_all[:, :kv_rank]).astype(jnp.bfloat16)
    rope_new = rope_rotate(kv_all[:, kv_rank:], angle_rad).astype(jnp.bfloat16)
    q_rope = rope_rotate(q_all[:, :, nope_dim:].astype(jnp.float32), angle_rad[:, None, :]).astype(jnp.bfloat16)
    q_lat = jnp.einsum('bhn,hnc->bhc', q_all[:, :, :nope_dim], w_ukey, preferred_element_type=jnp.float32).astype(jnp.bfloat16)
    seq_ids = jnp.arange(seq_len)
    at_pos = (seq_ids[None, :] == tok_pos[:, None])[:, :, None]
    lat_out = jnp.where(at_pos, lat_new[:, None, :], lat_cache)
    rope_out = jnp.where(at_pos, rope_new[:, None, :], rope_cache)
    scores = jnp.einsum('bhc,bsc->bhs', q_lat, lat_out, preferred_element_type=jnp.float32)
    scores = scores + jnp.einsum('bhr,bsr->bhs', q_rope, rope_out, preferred_element_type=jnp.float32)
    scores = scores * (nope_dim + rope_dim) ** -0.5
    visible = (seq_ids[None, :] <= tok_pos[:, None])[:, None, :]
    scores = jnp.where(visible, scores, -jnp.inf)
    prob_mat = jax.nn.softmax(scores, axis=-1).astype(jnp.bfloat16)
    o_lat = jnp.einsum('bhs,bsc->bhc', prob_mat, lat_out, preferred_element_type=jnp.float32).astype(jnp.bfloat16)
    o_heads = jnp.einsum('bhc,hcv->bhv', o_lat, w_uval, preferred_element_type=jnp.float32).astype(jnp.bfloat16)
    attn_out = jnp.dot(o_heads.reshape(tok_rows, -1), w_out, preferred_element_type=jnp.float32)
    resid_bf = (x_wide + attn_out).astype(jnp.bfloat16)
    h_norm = rms_norm(resid_bf.astype(jnp.float32), ffn_gain).astype(jnp.bfloat16)
    return resid_bf, h_norm, lat_out, rope_out


def route_weights(h_norm, w_router, expert_ids):
    num_experts = w_router.shape[1]
    gate_prob = jax.nn.sigmoid(jnp.dot(h_norm, w_router, preferred_element_type=jnp.float32))
    pick_mask = expert_ids[:, :, None] == jnp.arange(num_experts)[None, None, :]
    chosen = jnp.sum(jnp.where(pick_mask, gate_prob[:, None, :], 0.0), axis=-1)
    route_w = ROUTE_SCALE * chosen / jnp.sum(chosen, axis=1, keepdims=True)
    return route_w, pick_mask


def swiglu_shared(h_norm, sh_gate, sh_up, sh_down):
    gate_val = jnp.dot(h_norm, sh_gate, preferred_element_type=jnp.float32)
    up_val = jnp.dot(h_norm, sh_up, preferred_element_type=jnp.float32)
    act_val = (jax.nn.silu(gate_val) * up_val).astype(jnp.bfloat16)
    return jnp.dot(act_val, sh_down, preferred_element_type=jnp.float32)


def solution(mesh):
    ep_size = mesh.shape['ep']
    row_one = P(('dp', 'ep'))
    row_two = P(('dp', 'ep'), None)
    row_three = P(('dp', 'ep'), None, None)
    rep_one = P(None)
    rep_two = P(None, None)
    rep_three = P(None, None, None)
    exp_spec = P('ep', None, None)

    def local_step(tok_in, lat_cache, rope_cache, tok_pos, expert_ids, attn_gain, w_query, w_kvdown, w_ukey, w_uval, w_out, ffn_gain, w_router, sh_gate, sh_up, sh_down, ex_gate, ex_up, ex_down):
        resid_bf, h_norm, lat_out, rope_out = attention_block(tok_in, lat_cache, rope_cache, tok_pos, attn_gain, w_query, w_kvdown, w_ukey, w_uval, w_out, ffn_gain)
        route_w, pick_mask = route_weights(h_norm, w_router, expert_ids)
        shared_out = swiglu_shared(h_norm, sh_gate, sh_up, sh_down)
        tok_rows, top_k = expert_ids.shape
        num_experts = w_router.shape[1]
        local_experts = ex_gate.shape[0]
        d_model = h_norm.shape[1]
        cap_slots = max(2, -(-2 * tok_rows * top_k // num_experts))
        pick_int = pick_mask.astype(jnp.int32)
        per_tok = jnp.sum(pick_int, axis=1)
        before = jnp.cumsum(per_tok, axis=0) - per_tok
        slot_idx = jnp.sum(pick_int * before[:, None, :], axis=-1)
        slot_hot = slot_idx[:, :, None] == jnp.arange(cap_slots)
        place_hot = (pick_mask[:, :, :, None] & slot_hot[:, :, None, :]).astype(jnp.bfloat16)
        place_tok = jnp.sum(place_hot, axis=1)
        send_rows = jnp.einsum('tec,td->ecd', place_tok, h_norm, preferred_element_type=jnp.float32).astype(jnp.bfloat16)
        send_rows = send_rows.reshape(ep_size, local_experts, cap_slots, d_model)
        recv_rows = lax.all_to_all(send_rows, 'ep', 0, 2, tiled=True)
        recv_rows = recv_rows.reshape(local_experts, ep_size * cap_slots, d_model)
        gate_val = jnp.einsum('emd,edf->emf', recv_rows, ex_gate, preferred_element_type=jnp.float32)
        up_val = jnp.einsum('emd,edf->emf', recv_rows, ex_up, preferred_element_type=jnp.float32)
        act_val = (jax.nn.silu(gate_val) * up_val).astype(jnp.bfloat16)
        exp_out = jnp.einsum('emf,efd->emd', act_val, ex_down, preferred_element_type=jnp.float32).astype(jnp.bfloat16)
        exp_out = exp_out.reshape(1, local_experts, ep_size * cap_slots, d_model)
        back_rows = lax.all_to_all(exp_out, 'ep', 2, 0, tiled=True)
        back_rows = back_rows.reshape(num_experts, cap_slots, d_model)
        picked = jnp.einsum('tkec,ecd->tkd', place_hot, back_rows, preferred_element_type=jnp.float32)
        routed = jnp.sum(route_w[:, :, None] * picked, axis=1)
        out_hidden = (resid_bf.astype(jnp.float32) + shared_out + routed).astype(jnp.bfloat16)
        return out_hidden, lat_out, rope_out

    in_specs = (row_two, row_three, row_three, row_one, row_two, rep_one, rep_two, rep_two, rep_three, rep_three, rep_two, rep_one, rep_two, rep_two, rep_two, rep_two, exp_spec, exp_spec, exp_spec)
    out_specs = (row_two, row_three, row_three)
    return jax.shard_map(local_step, mesh=mesh, in_specs=in_specs, out_specs=out_specs, check_vma=False)
```

profile of v0, /device:TPU:15, one launch (start us, length us, event | category | flops | bytes accessed | tf_op | source)
XLA Modules:
  0.0 278.4 jit_solution(9962345916834524166)
XLA Ops:
  0.6 1.6 convert_reduce_fusion
  2.2 1.4 iota_compare_fusion
  4.2 1.3 iota_compare_fusion.3
  5.5 1.2 convert_element_type.96
  7.4 1.1 fusion.27
  9.1 7.1 %convolution_convert_fusion = bf16[64,3072]{1,0:T(8,128)(2,1)S(1)} fusion(bf16[2048,3072]{1,0:T(8,128)(2,1)} %param.25, bf16[64,2048]{1,0:T(8,128)(2,1)} %param.19, f32[2048]{0:T(1024)S(1)} %convert_element_type.89, f32[64]{0:T(128)S(1)} %add_rsqrt_fusion.2), kind=kOutput, calls=%fused_computation.5 | convolution fusion | flops 806027264 | bytes 13246720 | tf_op jit(solution)/shard_map/dot_general | solution.py:36
  17.6 1.0 slice_convert_fusion
  19.5 0.9 sub.25
  20.4 1.2 select_reduce_fusion.2
  21.6 1.5 fusion.39
  23.3 2.0 fusion.12
  25.4 0.9 broadcast_select_fusion
  26.3 1.2 fusion.25
  30.4 4.0 %convolution_convert_fusion.3 = bf16[64,16,512]{2,1,0:T(8,128)(2,1)S(1)} fusion(bf16[64,64,512]{2,1,0:T(8,128)(2,1)} %copy-done.2, f32[64,16]{1,0:T(8,128)S(1)} %fusion.46, f32[64,16,64]{2,1,0:T(8,128)S(1)} %fusion.15), kind=kOutput, calls=%fused_computation.22 | convolution fusion | flops 67830848 | bytes 5509120 | tf_op jit(solution)/shard_map/bhs,bsc->bhc/dot_general | solution.py:54
  34.5 2.9 %fusion.20 = bf16[16,8,8,128]{3,2,1,0:T(8,128)(2,1)S(1)} fusion(bf16[16,512,128]{2,1,0:T(8,128)(2,1)} %param.28, bf16[64,16,512]{2,1,0:T(8,128)(2,1)S(1)} %convolution_convert_fusion.3), kind=kOutput, calls=%fused_computation.34 | convolution fusion | flops 134348800 | bytes 3407872 | tf_op jit(solution)/shard_map/bhc,hcv->bhv/dot_general | solution.py:55
  37.4 5.1 %multiply_reduce_fusion = (f32[64]{0:T(128)S(1)}, f32[64,2048]{1,0:T(8,128)S(1)}) fusion(bf16[2048,2048]{1,0:T(8,128)(2,1)} %param.29, bf16[16,8,8,128]{3,2,1,0:T(8,128)(2,1)S(1)} %fusion.20, bf16[64,2048]{1,0:T(8,128)(2,1)S(1)} %copy-done.3), kind=kOutput, calls=%fused_computation.49 | convolution fusion | flops 537657280 | bytes 9437440 | tf_op jit(solution)/shard_map/dot_general | solution.py:56
  42.5 0.9 fusion.17
  43.4 2.7 convolution_convert_fusion.2
  46.1 5.7 %reshape.200 = bf16[16,4,12,2048]{3,1,0,2:T(4,128)(2,1)} reshape(bf16[64,12,2048]{2,0,1:T(8,128)(2,1)} %convolution_convert_fusion.2) | data formatting | bytes 6291456 | tf_op jit(solution)/shard_map/reshape | solution.py:105
  51.8 3.4 %copy.34 = bf16[16,4,12,2048]{3,1,2,0:T(4,128)(2,1)S(1)} copy(bf16[16,4,12,2048]{3,1,0,2:T(4,128)(2,1)} %reshape.200) | data formatting | bytes 6291456 | tf_op jit(solution)/shard_map/reshape | solution.py:105
  55.2 76.0 %all_to_all.30 = bf16[16,4,12,2048]{3,1,2,0:T(4,128)(2,1)S(1)} all-to-all(bf16[16,4,12,2048]{3,1,2,0:T(4,128)(2,1)S(1)} %copy.34), channel_id=1, replica_groups=mesh['dp'=2,'ep'=16] {'ep'}, dimensions={0} | all-to-all | bytes 6291456 | tf_op jit(solution)/shard_map/all_to_all | solution.py:106
  131.2 14.0 %fusion.6 = f32[4,192,1408]{2,1,0:T(8,128)} fusion(bf16[4,2048,1408]{2,1,0:T(8,128)(2,1)} %param.35, bf16[4,192,2048]{2,0,1:T(4,128)(2,1)S(1)} %bitcast.52), kind=kOutput, calls=%fused_computation.14 | convolution fusion | flops 4429185024 | bytes 30539776 | tf_op jit(solution)/shard_map/emd,edf->emf/dot_general | solution.py:108
  145.2 14.0 %multiply_convert_fusion = bf16[4,192,1408]{2,1,0:T(8,128)(2,1)} fusion(f32[4,192,1408]{2,1,0:T(8,128)} %fusion.6, bf16[4,2048,1408]{2,1,0:T(8,128)(2,1)} %param.36, bf16[4,192,2048]{2,0,1:T(4,128)(2,1)S(1)} %bitcast.53), kind=kOutput, calls=%fused_computation.1 | convolution fusion | flops 4435673088 | bytes 32702464 | tf_op jit(solution)/shard_map/emd,edf->emf/dot_general | solution.py:109
  159.2 11.1 %fusion.3 = bf16[1,4,192,2048]{3,2,1,0:T(8,128)(2,1)S(1)} fusion(bf16[4,192,1408]{2,1,0:T(8,128)(2,1)} %multiply_convert_fusion, bf16[4,1408,2048]{2,1,0:T(8,128)(2,1)} %param.37), kind=kOutput, calls=%fused_computation.10 | convolution fusion | flops 4430757888 | bytes 28377088 | tf_op jit(solution)/shard_map/emf,efd->emd/dot_general | solution.py:111
  170.3 4.1 %copy.37 = bf16[1,4,192,2048]{3,1,0,2:T(4,128)(2,1)} copy(bf16[1,4,192,2048]{3,2,1,0:T(8,128)(2,1)S(1)} %fusion.3) | data formatting | bytes 6291456 | tf_op jit(solution)/shard_map/reshape | solution.py:112
  174.4 5.4 %all-to-all-start.1 = ((bf16[1,4,192,2048]{3,1,0,2:T(4,128)(2,1)}), bf16[1,4,192,2048]{3,1,0,2:T(4,128)(2,1)}, u32[]{:S(2)}, u32[]{:S(2)}) async-start(bf16[1,4,192,2048]{3,1,0,2:T(4,128)(2,1)} %copy.37), calls=%async_computation.1 | async-start | bytes 6291456 | tf_op jit(solution)/shard_map/all_to_all | solution.py:113
  180.4 7.3 %fusion.45 = f32[64,2816]{1,0:T(8,128)} fusion(bf16[2048,2816]{1,0:T(8,128)(2,1)} %param.32, f32[64,2048]{1,0:T(8,128)S(1)} %get-tuple-element.16, f32[2048]{0:T(1024)S(1)} %convert_element_type.104, f32[64]{0:T(128)S(1)} %add_rsqrt_fusion), kind=kOutput, calls=%fused_computation.87 | convolution fusion | flops 738590720 | bytes 12787968 | tf_op jit(solution)/shard_map/dot_general | solution.py:72
  187.8 62.3 %all-to-all-done.1 = bf16[1,4,192,2048]{3,1,0,2:T(4,128)(2,1)} async-done(((bf16[1,4,192,2048]{3,1,0,2:T(4,128)(2,1)}), bf16[1,4,192,2048]{3,1,0,2:T(4,128)(2,1)}, u32[]{:S(2)}, u32[]{:S(2)}) %all-to-all-start.1) | async-done | bytes 3145760 | tf_op jit(solution)/shard_map/all_to_all | solution.py:113
  250.0 5.8 %copy.38 = bf16[16,1,4,12,2048]{4,2,0,3,1:T(4,128)(2,1)} copy(bf16[16,1,4,12,2048]{4,2,3,0,1:T(4,128)(2,1)} %bitcast.10) | data formatting | bytes 6291456 | tf_op jit(solution)/shard_map/all_to_all | solution.py:113
  255.8 5.5 %reshape.205 = bf16[64,12,2048,1]{2,0,1,3:T(8,128)(2,1)} reshape(bf16[16,1,4,12,2048]{4,2,0,3,1:T(4,128)(2,1)} %copy.38) | data formatting | bytes 6291456 | tf_op jit(solution)/shard_map/reshape | solution.py:114
  261.3 4.2 %fusion.2 = f32[64,2048]{1,0:T(8,128)S(1)} fusion(bf16[64,12,2048,1]{2,0,1,3:T(8,128)(2,1)} %reshape.205, f32[64,6]{0,1:T(8,128)S(1)} %multiply_divide_fusion, pred[64,6,12]{0,2,1:T(8,128)(4,1)S(1)} %iota_compare_fusion.1, pred[64,6,64]{2,0,1:T(8,128)(4,1)S(1)} %copy-done.9), kind=kOutput, calls=%fused_computation.9 | convolution fusion | flops 1209696256 | bytes 3700736 | tf_op jit(solution)/shard_map/tkec,ecd->tkd/dot_general | solution.py:115
  265.6 12.9 %fusion.11 = bf16[64,2048]{1,0:T(8,128)(2,1)} fusion(f32[64,2048]{1,0:T(8,128)S(1)} %fusion.2, f32[64,2048]{1,0:T(8,128)S(1)} %get-tuple-element.16, bf16[2816,2048]{1,0:T(8,128)(2,1)} %param.34, bf16[2048,2816]{1,0:T(8,128)(2,1)} %param.33, f32[64,2816]{1,0:T(8,128)} %fusion.45, f32[2048]{0:T(1024)S(1)} %convert_element_type.104, f32[64]{0:T(128)S(1)} %add_rsqrt_fusion), kind=kOutput, calls=%fused_computation.21 | convolution fusion | flops 1478262784 | bytes 25108736 | tf_op jit(solution)/shard_map/dot_general | solution.py:75
  (54 shorter events, 7.7 us)
Async XLA Ops:
  0.6 20.9 %copy-start = (bf16[2048,576]{0,1:T(8,128)(2,1)S(1)}, bf16[2048,576]{0,1:T(8,128)(2,1)}, u32[]{:S(2)}) copy-start(bf16[2048,576]{0,1:T(8,128)(2,1)} %param.26) | copy-start | bytes 7077892
  8.5 0.6 copy-start.12
  9.1 12.5 %copy-start.3 = (bf16[64,2048]{1,0:T(8,128)(2,1)S(1)}, bf16[64,2048]{1,0:T(8,128)(2,1)}, u32[]{:S(2)}) copy-start(bf16[64,2048]{1,0:T(8,128)(2,1)} %param.19) | copy-start | bytes 786436
  16.8 0.8 copy-start.6
  17.6 5.7 %slice-start = ((bf16[64,16,192]{2,1,0:T(8,128)(2,1)}), bf16[64,16,128]{2,1,0:T(8,128)(2,1)S(1)}, s32[]{:S(2)}) async-start(bf16[64,16,192]{2,1,0:T(8,128)(2,1)} %copy-done.6), calls=%async_computation.2 | async-start | bytes 524288 | tf_op jit(solution)/shard_map/slice | solution.py:43
  19.5 5.9 %copy-start.4 = (bf16[64,64,512]{2,1,0:T(8,128)(2,1)S(1)}, bf16[64,64,512]{2,1,0:T(8,128)(2,1)}, u32[]{:S(2)}) copy-start(bf16[64,64,512]{2,1,0:T(8,128)(2,1)} %param.20) | copy-start | bytes 12582916
  26.3 3.0 %copy-start.2 = (bf16[64,64,512]{2,1,0:T(8,128)(2,1)}, bf16[64,64,512]{2,1,0:T(8,128)(2,1)S(1)}, u32[]{:S(2)}) copy-start(bf16[64,64,512]{2,1,0:T(8,128)(2,1)S(1)} %broadcast_select_fusion) | copy-start | bytes 12582916
  26.3 1.2 copy-start.14
  26.3 1.2 copy-start.15
  26.3 2.0 copy-start.7
  26.3 3.0 %copy-start.11 = (pred[64,64]{1,0:T(8,128)(4,1)S(1)}, pred[64,64]{1,0:T(8,128)(4,1)}, u32[]{:S(2)}) copy-start(pred[64,64]{1,0:T(8,128)(4,1)} %get-tuple-element.13) | copy-start | bytes 12292
  29.0 5.4 %copy-start.5 = (bf16[64,64,64]{2,1,0:T(8,128)(2,1)}, bf16[64,64,64]{2,1,0:T(8,128)(2,1)S(1)}, u32[]{:S(2)}) copy-start(bf16[64,64,64]{2,1,0:T(8,128)(2,1)S(1)} %broadcast_select_fusion.1) | copy-start | bytes 1572868
  29.3 5.1 %copy-start.13 = (bf16[2048]{0:T(1024)(128)(2,1)S(1)}, bf16[2048]{0:T(1024)(128)(2,1)}, u32[]{:S(2)}) copy-start(bf16[2048]{0:T(1024)(128)(2,1)} %param.30) | copy-start | bytes 12292
  37.4 5.1 %copy-start.9 = (pred[64,6,64]{2,0,1:T(8,128)(4,1)S(1)}, pred[64,6,64]{2,0,1:T(8,128)(4,1)}, u32[]{:S(2)}) copy-start(pred[64,6,64]{2,0,1:T(8,128)(4,1)} %iota_compare_fusion) | copy-start | bytes 73732
  174.4 5.4 %copy-start.8 = (bf16[2048,64]{0,1:T(8,128)(2,1)S(1)}, bf16[2048,64]{0,1:T(8,128)(2,1)}, u32[]{:S(2)}) copy-start(bf16[2048,64]{0,1:T(8,128)(2,1)} %param.31) | copy-start | bytes 786436
  174.4 5.7 %copy-start.10 = (s32[64,6]{0,1:T(8,128)S(1)}, s32[64,6]{0,1:T(8,128)}, u32[]{:S(2)}) copy-start(s32[64,6]{0,1:T(8,128)} %param.23) | copy-start | bytes 4612
  174.4 75.6 %all-to-all-start.1 = ((bf16[1,4,192,2048]{3,1,0,2:T(4,128)(2,1)}), bf16[1,4,192,2048]{3,1,0,2:T(4,128)(2,1)}, u32[]{:S(2)}, u32[]{:S(2)}) async-start(bf16[1,4,192,2048]{3,1,0,2:T(4,128)(2,1)} %copy.37), calls=%async_computation.1 | async-start | bytes 6291456 | tf_op jit(solution)/shard_map/all_to_all | solution.py:113
  265.5 12.9 %copy-start.1 = (bf16[2048,576]{0,1:T(8,128)(2,1)S(1)}, bf16[2048,576]{0,1:T(8,128)(2,1)}, u32[]{:S(2)}) copy-start(bf16[2048,576]{0,1:T(8,128)(2,1)} %param.26) | copy-start | bytes 7077892
where the time goes:
time: 279 us; the launch traced here: 278 us
  matrix products  91 us (33%)
  blocking collectives  76 us (27%)
  waiting for transfers between devices  62.3 us (22%)
  local copies, waits for them, and re-layouts  27.1 us (10%)
  other arithmetic  15.7 us (6%)
  starting transfers between devices  5.41 us (2%)
    all_to_all x1, blocking collectives, local_step(): recv_rows = lax.all_to_all(send_rows, 'ep', 0, 2, tiled=True)  76 us
    all_to_all x1, waiting for transfers between devices, local_step(): back_rows = lax.all_to_all(exp_out, 'ep', 2, 0, tiled=True)  62.3 us
    dot_general x1, matrix products, local_step(): jnp.einsum('emd,edf->emf', recv_rows, ex_up, preferred_element_type=jnp.f...  14 us
    dot_general x1, matrix products, local_step(): jnp.einsum('emd,edf->emf', recv_rows, ex_gate, preferred_element_type=jnp...  14 us
    dot_general x1, matrix products, swiglu_shared(): return jnp.dot(act_val, sh_down, preferred_element_type=jnp.float32)  12.9 us
    dot_general x1, matrix products, local_step(): jnp.einsum('emf,efd->emd', act_val, ex_down, preferred_element_type=jnp.f...  11.1 us
    reshape x2, local copies, waits for them, and re-layouts, local_step(): send_rows = send_rows.reshape(ep_size, local_experts, cap_slots, d_model)  9.12 us
    dot_general x1, matrix products, swiglu_shared(): gate_val = jnp.dot(h_norm, sh_gate, preferred_element_type=jnp.float32)  7.32 us
  transfers between devices with their start and end apart: 1, of which 1 were waited for; matrix products, arithmetic and copies ran while one was open for 3% of the time, Pallas kernels for 0%

commit v1 on v0

v1 whole, which is shorter than its diff:
```python
import jax
import jax.numpy as jnp
from jax import lax
from jax.experimental import pallas as pl
from jax.experimental.pallas import tpu as pltpu
from jax.sharding import PartitionSpec as P

ROUTE_SCALE = 2.827
ROPE_BASE = 10000.0
NORM_EPS = 1e-6


def unit_norm(values):
    mean_sq = jnp.mean(jnp.square(values), axis=-1, keepdims=True)
    return values * lax.rsqrt(mean_sq + NORM_EPS)


def rms_norm(values, gain_vec):
    return unit_norm(values) * gain_vec.astype(jnp.float32)


def rope_rotate(values, angle_rad):
    half_dim = values.shape[-1] // 2
    x_first = values[..., :half_dim]
    x_second = values[..., half_dim:]
    cos_part = jnp.cos(angle_rad)
    sin_part = jnp.sin(angle_rad)
    return jnp.concatenate([x_first * cos_part - x_second * sin_part, x_second * cos_part + x_first * sin_part], axis=-1)


def attention_block(tok_in, lat_cache, rope_cache, tok_pos, attn_gain, w_query, w_kvdown, w_ukey, w_uval, w_out, ffn_gain):
    num_heads, nope_dim, kv_rank = w_ukey.shape
    rope_dim = rope_cache.shape[-1]
    seq_len = lat_cache.shape[1]
    tok_rows = tok_in.shape[0]
    x_wide = tok_in.astype(jnp.float32)
    x_norm = rms_norm(x_wide, attn_gain).astype(jnp.bfloat16)
    q_all = jnp.dot(x_norm, w_query, preferred_element_type=jnp.float32).astype(jnp.bfloat16).reshape(tok_rows, num_heads, nope_dim + rope_dim)
    kv_all = jnp.dot(x_norm, w_kvdown, preferred_element_type=jnp.float32)
    inv_freq = ROPE_BASE ** (-(2.0 * jnp.arange(rope_dim // 2)) / rope_dim)
    angle_rad = tok_pos.astype(jnp.float32)[:, None] * inv_freq[None, :]
    lat_new = unit_norm(kv_all[:, :kv_rank]).astype(jnp.bfloat16)
    rope_new = rope_rotate(kv_all[:, kv_rank:], angle_rad).astype(jnp.bfloat16)
    q_rope = rope_rotate(q_all[:, :, nope_dim:].astype(jnp.float32), angle_rad[:, None, :]).astype(jnp.bfloat16)
    q_lat = jnp.einsum('bhn,hnc->bhc', q_all[:, :, :nope_dim], w_ukey, preferred_element_type=jnp.float32).astype(jnp.bfloat16)
    seq_ids = jnp.arange(seq_len)
    at_pos = (seq_ids[None, :] == tok_pos[:, None])[:, :, None]
    lat_out = jnp.where(at_pos, lat_new[:, None, :], lat_cache)
    rope_out = jnp.where(at_pos, rope_new[:, None, :], rope_cache)
    scores = jnp.einsum('bhc,bsc->bhs', q_lat, lat_out, preferred_element_type=jnp.float32)
    scores = scores + jnp.einsum('bhr,bsr->bhs', q_rope, rope_out, preferred_element_type=jnp.float32)
    scores = scores * (nope_dim + rope_dim) ** -0.5
    visible = (seq_ids[None, :] <= tok_pos[:, None])[:, None, :]
    scores = jnp.where(visible, scores, -jnp.inf)
    prob_mat = jax.nn.softmax(scores, axis=-1).astype(jnp.bfloat16)
    o_lat = jnp.einsum('bhs,bsc->bhc', prob_mat, lat_out, preferred_element_type=jnp.float32).astype(jnp.bfloat16)
    o_heads = jnp.einsum('bhc,hcv->bhv', o_lat, w_uval, preferred_element_type=jnp.float32).astype(jnp.bfloat16)
    attn_out = jnp.dot(o_heads.reshape(tok_rows, -1), w_out, preferred_element_type=jnp.float32)
    resid_bf = (x_wide + attn_out).astype(jnp.bfloat16)
    h_norm = rms_norm(resid_bf.astype(jnp.float32), ffn_gain).astype(jnp.bfloat16)
    return resid_bf, h_norm, lat_out, rope_out


MESH = pl.DeviceIdType.MESH
NE = 4
CAP = 12
SRC = 4
GRP = SRC * CAP
NCH = 8
NA = 4
NB = 4
AHEAD = 2


def moe_kernel(hx_ref, res_ref, rtr_ref, sg_hbm, su_hbm, sd_hbm, eg_hbm, eu_hbm, ed_hbm, out_ref,
               hall, xbuf, act, sact, sout, abuf, bbuf, sbuf, rbuf, fbuf, zbuf, rly, w3,
               a_sem, b_sem, zup_s, zdn_s, z_r, y_s, y_r, c_s, c_r, s_s, s_r, f_s, f_r, l_s, l_r):
    f32, bf16 = jnp.float32, jnp.bfloat16
    dm = res_ref.shape[1]
    rows = res_ref.shape[0]
    ff = act.shape[2]
    cw = dm // NCH
    me = lax.axis_index("ep")
    z, q = me // 4, me % 4
    qy = jnp.where(q >= 2, q - 2, q + 2)
    qc = jnp.where(q % 2 == 1, q - 1, q + 1)
    qd = 3 - q
    peers = (qc, qy, qd)

    def dev(zz, qq):
        return {"ep": zz * 4 + qq}

    def a_src(u):
        if u < 4:
            return (sg_hbm, su_hbm)[u % 2].at[:, pl.ds((u // 2) * ff, ff)]
        return (eg_hbm, eu_hbm)[u % 2].at[(u - 4) // 2]

    def a_copy(u):
        return pltpu.make_async_copy(a_src(u), abuf.at[u % NA], a_sem.at[u % NA])

    def sd_copy(p, hf):
        return pltpu.make_async_copy(sd_hbm.at[:, :, pl.ds((2 * p + hf) * cw, cw)], bbuf.at[p, pl.ds(2 * hf, 2)], b_sem.at[p, hf])

    def b_copy(cc):
        return pltpu.make_async_copy(ed_hbm.at[:, :, pl.ds(cc * cw, cw)], bbuf.at[cc % NB], b_sem.at[cc % NB, 0])

    for u in range(NA):
        a_copy(u).start()
    for p in range(NCH // 2):
        for hf in range(2):
            sd_copy(p, hf).start()

    bar = pltpu.get_barrier_semaphore()
    for s in range(1, 4):
        pl.semaphore_signal(bar, inc=1, device_id=dev((z + s) % 4, q), device_id_type=MESH)
    for qq in peers:
        pl.semaphore_signal(bar, inc=1, device_id=dev(z, qq), device_id_type=MESH)
    pl.semaphore_wait(bar, 6)

    def rcopy(src, dst, ss, rs, d):
        return pltpu.make_async_remote_copy(src_ref=src, dst_ref=dst, send_sem=ss, recv_sem=rs, device_id=d, device_id_type=MESH)

    def up(src, b):
        return rcopy(src, hall.at[q, b], zup_s.at[b], z_r.at[b], dev(z + 1, q))

    def dn(src, b):
        return rcopy(src, hall.at[q, b], zdn_s.at[b], z_r.at[b], dev(z - 1, q))

    def ysend(src, b):
        return rcopy(src, hall.at[q, b], y_s.at[b], y_r.at[b], dev(z, qy))

    def yrecv(b):
        return rcopy(hall.at[qy, b], hall.at[qy, b], y_s.at[b], y_r.at[b], dev(z, qy))

    def csend(src, qq, k, b):
        return rcopy(src, hall.at[qq, b], c_s.at[k, b], c_r.at[k, b], dev(z, qc))

    @pl.when(z < 3)
    def _():
        up(hx_ref, z).start()

    @pl.when(z > 0)
    def _():
        dn(hx_ref, z).start()

    ysend(hx_ref, z).start()
    csend(hx_ref, q, 0, z).start()
    hall[q, z] = hx_ref[...]

    def gather_step(s):
        if s <= 3:
            @pl.when(z - s >= 0)
            def _():
                b = z - s
                up(hall.at[q, b], b).wait_recv()

                @pl.when(z < 3)
                def _():
                    up(hall.at[q, b], b).start()
                ysend(hall.at[q, b], b).start()
                csend(hall.at[q, b], q, 0, b).start()

            @pl.when(z + s <= 3)
            def _():
                b = z + s
                dn(hall.at[q, b], b).wait_recv()

                @pl.when(z > 0)
                def _():
                    dn(hall.at[q, b], b).start()
                ysend(hall.at[q, b], b).start()
                csend(hall.at[q, b], q, 0, b).start()
        t = s - 1
        for sign in ((1, -1) if t else (1,)):
            b = z - sign * t

            @pl.when((b >= 0) & (b <= 3))
            def _():
                yrecv(b).wait_recv()
                csend(hall.at[qy, b], qy, 1, b).start()

    def dot(a, b):
        return jnp.dot(a, b, preferred_element_type=f32)

    def gate_up(x, sg, su, store):
        def tile(off, width):
            g = dot(x(), abuf[sg, :, pl.ds(off, width)])
            u = dot(x(), abuf[su, :, pl.ds(off, width)])
            store(off, width, (g * jax.nn.sigmoid(g) * u).astype(bf16))

        def body(n, carry):
            tile(pl.multiple_of(n * 256, 256), 256)
            return carry
        lax.fori_loop(0, ff // 256, body, 0)
        if ff % 256:
            tile(ff - ff % 256, ff % 256)

    for j in range(2):
        a_copy(2 * j).wait()
        a_copy(2 * j + 1).wait()

        def put(off, width, v, j=j):
            sact[j, :, pl.ds(off, width)] = v
        gate_up(lambda: hx_ref[:, pl.ds(0, dm)], (2 * j) % NA, (2 * j + 1) % NA, put)
        for u in (2 * j + NA, 2 * j + NA + 1):
            a_copy(u).start()
        gather_step(j + 1)
    for p in range(NCH // 2):
        for hf in range(2):
            sd_copy(p, hf).wait()
            sout[2 * p + hf] = dot(sact[0], bbuf[p, 2 * hf]) + dot(sact[1], bbuf[p, 2 * hf + 1])
        b_copy(p).start()
    gather_step(3)

    def spread():
        ee = lax.broadcasted_iota(jnp.int32, (128, SRC * NE * GRP), 0)
        col = lax.broadcasted_iota(jnp.int32, (1, SRC * NE * GRP), 1)
        col48 = lax.rem(col, GRP)
        col_z = lax.div(col48, CAP)
        col_k = (lax.rem(col48, CAP) + 1).astype(f32)
        blk = lax.div(col, NE * GRP)
        owner = jnp.where(blk == 0, q, jnp.where(blk == 1, qc, jnp.where(blk == 2, qy, qd)))
        rep = (ee == SRC * NE * z + NE * owner + lax.div(lax.rem(col, NE * GRP), GRP)).astype(f32).astype(bf16)
        for b in range(SRC):
            hz = hall[q, b, :, pl.ds(0, dm)]
            code = hall[q, b, :, pl.ds(dm, 128)]
            s = jax.nn.sigmoid(dot(hz, rtr_ref[...]))
            chosen = jnp.where(code.astype(f32) > 0.0, s, 0.0)
            w = ROUTE_SCALE * chosen / jnp.sum(chosen, axis=1, keepdims=True)
            hi = w.astype(bf16)
            r1 = w - hi.astype(f32)
            mid = r1.astype(bf16)
            low = (r1 - mid.astype(f32)).astype(bf16)
            ok = (dot(code, rep) == col_k) & (col_z == b)
            for i, part in enumerate((hi, mid, low)):
                w3[i, pl.ds(b * rows, rows)] = jnp.where(ok, dot(part, rep), 0.0).astype(bf16)

    def select(g):
        nr = NE * GRP
        ee = lax.broadcasted_iota(jnp.int32, (nr, 128), 1)
        ri = lax.broadcasted_iota(jnp.int32, (nr, 128), 0)
        lo = (ee - NE * me) * GRP
        sel = ((ri >= lo) & (ri < lo + GRP)).astype(f32).astype(bf16)
        rcol = lax.broadcasted_iota(jnp.int32, (nr, 1), 0)
        r48 = lax.rem(rcol, GRP)
        row_z = lax.div(r48, CAP)
        row_k = (lax.rem(r48, CAP) + 1).astype(f32)
        code = hall[g, :, :, pl.ds(dm, 128)].reshape(SRC * rows, 128)
        ct = lax.dot_general(sel, code, (((1,), (1,)), ((), ())), preferred_element_type=f32)
        tz = lax.div(lax.broadcasted_iota(jnp.int32, (1, SRC * rows), 1), rows)
        pick = jnp.where((ct == row_k) & (row_z == tz), 1.0, 0.0).astype(bf16)

        def body(n, carry):
            off = pl.multiple_of(n * 512, 512)
            hz = hall[g, :, :, pl.ds(off, 512)].reshape(SRC * rows, 512)
            x = dot(pick, hz).astype(bf16)
            for i in range(NE):
                xbuf[i, g, :, pl.ds(off, 512)] = x[i * GRP:(i + 1) * GRP]
            return carry
        lax.fori_loop(0, dm // 512, body, 0)

    spread()
    select(q)
    gather_step(4)
    select(qy)
    for k, qq in ((0, qc), (1, qd)):
        for b in range(SRC):
            rcopy(hall.at[qq, b], hall.at[qq, b], c_s.at[k, b], c_r.at[k, b], dev(z, qc)).wait_recv()
        select(qq)

    for i in range(NE):
        u = 4 + 2 * i
        a_copy(u).wait()
        a_copy(u + 1).wait()

        def put(off, width, v, i=i):
            act[i, :, pl.ds(off, width)] = v
        gate_up(lambda i=i: xbuf[i].reshape(SRC * GRP, dm), u % NA, (u + 1) % NA, put)
        for v in (u + NA, u + NA + 1):
            if v < 4 + 2 * NE:
                a_copy(v).start()

    def s_copy(cc, j):
        return rcopy(sbuf.at[cc, peers[j]], rbuf.at[cc, j], s_s.at[cc, j], s_r.at[cc, j], dev(z, peers[j]))

    def down(cc):
        b_copy(cc).wait()
        for i in range(NE):
            o = dot(act[i], bbuf[cc % NB, i]).astype(bf16)
            for g in range(4):
                sbuf[cc, g, pl.ds(i * GRP, GRP)] = o[g * GRP:(g + 1) * GRP]
        for j in (2, 1, 0):
            s_copy(cc, j).start()
        if cc + NB < NCH:
            b_copy(cc + NB).start()

    edge = (z == 0) | (z == 3)
    z_edge = jnp.where(z <= 1, 0, 3)
    z_mid = jnp.where(z <= 1, 1, 2)
    z_mid2 = 3 - z_mid
    z_edge2 = 3 - z_edge

    def f_copy(cc, dst_z, k, rk):
        return rcopy(fbuf.at[cc, dst_z], zbuf.at[cc, rk], f_s.at[cc, k], f_r.at[cc, rk], dev(dst_z, q))

    def l_copy(cc):
        return rcopy(fbuf.at[cc, z_edge2], rly.at[cc], l_s.at[cc], l_r.at[cc], dev(z_mid, q))

    def combine(cc):
        for j in range(3):
            s_copy(cc, j).wait_recv()
        got = jnp.concatenate([sbuf[cc, q]] + [rbuf[cc, j] for j in range(3)], axis=0)
        acc = dot(w3[0], got) + (dot(w3[1], got) + dot(w3[2], got))
        fbuf[cc] = acc.reshape(SRC, rows, cw)

        @pl.when(edge)
        def _():
            l_copy(cc).start()
            f_copy(cc, z_mid2, 1, 2).start()
            f_copy(cc, z_mid, 0, 0).start()

        @pl.when(jnp.logical_not(edge))
        def _():
            f_copy(cc, z_mid2, 1, 1).start()
            f_copy(cc, z_edge, 0, 0).start()

    def relay(cc):
        @pl.when(jnp.logical_not(edge))
        def _():
            l_copy(cc).wait_recv()
            fbuf[cc, z_edge2] += rly[cc]
            f_copy(cc, z_edge2, 2, 1).start()

    def final(cc):
        @pl.when(edge)
        def _():
            for rk in range(2):
                f_copy(cc, z_mid, 0, rk).wait_recv()
            cols = pl.ds(cc * cw, cw)
            out_ref[:, cols] = (res_ref[:, cols].astype(f32) + sout[cc] + (fbuf[cc, z] + zbuf[cc, 0] + zbuf[cc, 1])).astype(bf16)

        @pl.when(jnp.logical_not(edge))
        def _():
            for rk in range(3):
                f_copy(cc, z_mid, 0, rk).wait_recv()
            cols = pl.ds(cc * cw, cw)
            out_ref[:, cols] = (res_ref[:, cols].astype(f32) + sout[cc] + (fbuf[cc, z] + zbuf[cc, 0] + zbuf[cc, 1] + zbuf[cc, 2])).astype(bf16)

    for cc in range(AHEAD):
        down(cc)
    for cc in range(NCH):
        if cc + AHEAD < NCH:
            down(cc + AHEAD)
        combine(cc)
        if cc:
            relay(cc - 1)
    relay(NCH - 1)
    for cc in range(NCH):
        final(cc)

    @pl.when(z < 3)
    def _():
        up(hx_ref, z).wait_send()

    @pl.when(z > 0)
    def _():
        dn(hx_ref, z).wait_send()

    for s in range(1, 4):
        @pl.when((z - s >= 0) & (z < 3))
        def _():
            up(hall.at[q, z - s], z - s).wait_send()

        @pl.when((z + s <= 3) & (z > 0))
        def _():
            dn(hall.at[q, z + s], z + s).wait_send()
    for b in range(SRC):
        ysend(hall.at[q, b], b).wait_send()
        csend(hall.at[q, b], q, 0, b).wait_send()
        csend(hall.at[qy, b], qy, 1, b).wait_send()
    for cc in range(NCH):
        for j in range(3):
            s_copy(cc, j).wait_send()
        f_copy(cc, z_mid, 0, 0).wait_send()
        f_copy(cc, z_mid, 1, 0).wait_send()

        @pl.when(edge)
        def _():
            l_copy(cc).wait_send()

        @pl.when(jnp.logical_not(edge))
        def _():
            f_copy(cc, z_edge2, 2, 1).wait_send()


def moe_call(hx, resid, router, sh_gate, sh_up, sh_down, ex_gate, ex_up, ex_down):
    rows, dm = resid.shape
    ff = ex_gate.shape[2]
    cw = dm // NCH
    bf16, f32 = jnp.bfloat16, jnp.float32
    vm = pl.BlockSpec(memory_space=pltpu.VMEM)
    hb = pl.BlockSpec(memory_space=pl.ANY)
    sem = pltpu.SemaphoreType.DMA
    nk = NE * GRP
    return pl.pallas_call(
        moe_kernel,
        out_shape=jax.ShapeDtypeStruct((rows, dm), bf16),
        in_specs=[vm] * 3 + [hb] * 6,
        out_specs=vm,
        scratch_shapes=[
            pltpu.VMEM((4, SRC, rows, dm + 128), bf16),
            pltpu.VMEM((NE, 4, GRP, dm), bf16),
            pltpu.VMEM((NE, SRC * GRP, ff), bf16),
            pltpu.VMEM((2, rows, ff), bf16),
            pltpu.VMEM((NCH, rows, cw), f32),
            pltpu.VMEM((NA, dm, ff), bf16),
            pltpu.VMEM((NB, NE, ff, cw), bf16),
            pltpu.VMEM((NCH, 4, nk, cw), bf16),
            pltpu.VMEM((NCH, 3, nk, cw), bf16),
            pltpu.VMEM((NCH, SRC, rows, cw), f32),
            pltpu.VMEM((NCH, 3, rows, cw), f32),
            pltpu.VMEM((NCH, rows, cw), f32),
            pltpu.VMEM((3, SRC * rows, SRC * nk), bf16),
            sem((NA,)), sem((NB, 2)),
            sem((4,)), sem((4,)), sem((4,)),
            sem((4,)), sem((4,)),
            sem((2, 4)), sem((2, 4)),
            sem((NCH, 3)), sem((NCH, 3)),
            sem((NCH, 3)), sem((NCH, 3)),
            sem((NCH,)), sem((NCH,)),
        ],
        compiler_params=pltpu.CompilerParams(collective_id=0, has_side_effects=True, vmem_limit_bytes=66 * 1024 * 1024 - 2 * 1024 * 1024 - 65536),
        name="moe",
    )(hx, resid, router, sh_gate, sh_up, sh_down.reshape(2, ff, dm), ex_gate, ex_up, ex_down)


def solution(mesh):
    row_one = P(('dp', 'ep'))
    row_two = P(('dp', 'ep'), None)
    row_three = P(('dp', 'ep'), None, None)
    rep_one = P(None)
    rep_two = P(None, None)
    rep_three = P(None, None, None)
    exp_spec = P('ep', None, None)

    def local_step(tok_in, lat_cache, rope_cache, tok_pos, expert_ids, attn_gain, w_query, w_kvdown, w_ukey, w_uval, w_out, ffn_gain, w_router, sh_gate, sh_up, sh_down, ex_gate, ex_up, ex_down):
        resid_bf, h_norm, lat_out, rope_out = attention_block(tok_in, lat_cache, rope_cache, tok_pos, attn_gain, w_query, w_kvdown, w_ukey, w_uval, w_out, ffn_gain)
        num_experts = w_router.shape[1]
        pick = (expert_ids[:, :, None] == jnp.arange(num_experts)[None, None, :]).astype(jnp.int32)
        per_tok = jnp.sum(pick, axis=1)
        code = (per_tok * jnp.cumsum(per_tok, axis=0)).astype(jnp.bfloat16)
        hx = jnp.concatenate([h_norm, jnp.pad(code, ((0, 0), (0, 128 - num_experts)))], axis=1)
        router = jnp.pad(w_router, ((0, 0), (0, 128 - num_experts)))
        out_hidden = moe_call(hx, resid_bf, router, sh_gate, sh_up, sh_down, ex_gate, ex_up, ex_down)
        return out_hidden, lat_out, rope_out

    in_specs = (row_two, row_three, row_three, row_one, row_two, rep_one, rep_two, rep_two, rep_three, rep_three, rep_two, rep_one, rep_two, rep_two, rep_two, rep_two, exp_spec, exp_spec, exp_spec)
    out_specs = (row_two, row_three, row_three)
    return jax.shard_map(local_step, mesh=mesh, in_specs=in_specs, out_specs=out_specs, check_vma=False)
```

time: 279 us -> 143 us (0.51)
  the two profiles are of different devices: /device:TPU:15 before, /device:TPU:0 now
where the time goes in v1:
time: 143 us; the launch traced here: 142 us
  Pallas kernels  100 us (70%)
  matrix products  26.3 us (18%)
  other arithmetic  10.1 us (7%)
  local copies, waits for them, and re-layouts  4.89 us (3%)
    pallas_call x1, Pallas kernels, moe_call(): pl.pallas_call(moe_kernel, out_shape=jax.ShapeDtypeStruct((rows, dm), bf1...  100 us
    dot_general x1, matrix products, attention_block(): jnp.dot(x_norm, w_query, preferred_element_type=jnp.float32)  7.09 us
    dot_general x1, matrix products, attention_block(): jnp.dot(o_heads.reshape(tok_rows, -1), w_out, preferred_element_type=jnp....  5.12 us
    dot_general x1, matrix products, attention_block(): jnp.einsum('bhs,bsc->bhc', prob_mat, lat_out, preferred_element_type=jnp....  4.04 us
    select_n x1, other arithmetic, attention_block(): lat_out = jnp.where(at_pos, lat_new[:, None, :], lat_cache)  3.99 us
    dot_general x1, matrix products, attention_block(): jnp.einsum('bhc,bsc->bhs', q_lat, lat_out, preferred_element_type=jnp.flo...  3.38 us
    unnamed x18, local copies, waits for them, and re-layouts  3.34 us
    dot_general x1, matrix products, attention_block(): jnp.einsum('bhc,hcv->bhv', o_lat, w_uval, preferred_element_type=jnp.floa...  2.93 us

profile of v1, /device:TPU:0, one launch (start us, length us, event | category | flops | bytes accessed | tf_op | source)
XLA Modules:
  0.0 142.2 jit_solution(9821533526391255537)
XLA Ops:
  0.6 0.8 convert_reduce_fusion
  1.4 0.1 reduce_window_sum.11
  1.6 0.7 iota_compare_fusion.3
  2.3 0.7 convert_element_type.75
  3.0 1.1 fusion.15
  4.1 2.6 %fusion.26 = f32[64,576]{1,0:T(8,128)S(1)} fusion(bf16[2048,576]{0,1:T(8,128)(2,1)} %param.26, bf16[64,2048]{1,0:T(8,128)(2,1)} %param.19, f32[2048]{0:T(1024)S(1)} %convert_element_type.75, f32[64]{0:T(128)S(1)} %add_rsqrt_fusion.2), kind=kOutput, calls=%fused_computation.47 | convolution fusion | flops 151519232 | bytes 2777344 | tf_op jit(solution)/shard_map/dot_general | solution.py:39
  6.7 0.1 multiply_reduce_fusion
  6.8 0.1 multiply_convert_fusion
  6.9 4.0 %broadcast_select_fusion = bf16[64,64,512]{2,1,0:T(8,128)(2,1)} fusion(bf16[64,64,512]{2,1,0:T(8,128)(2,1)} %param.20, pred[64,64]{1,0:T(8,128)(4,1)S(1)} %get-tuple-element.12, bf16[64,512]{1,0:T(8,128)(2,1)S(1)} %multiply_convert_fusion), kind=kLoop, calls=%fused_computation.1 | loop fusion | flops 2097152 | bytes 8458240 | tf_op jit(solution)/shard_map/jit(_where)/select_n | solution.py:48
  10.9 7.1 %convolution_convert_fusion = bf16[64,3072]{1,0:T(8,128)(2,1)S(1)} fusion(bf16[2048,3072]{1,0:T(8,128)(2,1)} %param.25, bf16[64,2048]{1,0:T(8,128)(2,1)S(1)} %copy-done, f32[2048]{0:T(1024)S(1)} %convert_element_type.75, f32[64]{0:T(128)S(1)} %add_rsqrt_fusion.2), kind=kOutput, calls=%fused_computation.2 | convolution fusion | flops 806027264 | bytes 13246720 | tf_op jit(solution)/shard_map/dot_general | solution.py:38
  18.0 0.6 reshape.151
  18.7 0.4 fusion.2
  19.2 3.4 %fusion.9 = f32[64,16,64]{2,1,0:T(8,128)S(1)} fusion(bf16[64,64,512]{2,1,0:T(8,128)(2,1)} %broadcast_select_fusion, bf16[64,16,512]{2,0,1:T(8,128)(2,1)S(1)} %fusion.2), kind=kOutput, calls=%fused_computation.16 | convolution fusion | flops 67108864 | bytes 5505024 | tf_op jit(solution)/shard_map/bhc,bsc->bhs/dot_general | solution.py:50
  22.6 0.0 copy-done.7
  22.6 0.2 multiply_cosine_fusion
  22.8 0.1 pad_maximum_fusion
  22.9 0.7 broadcast_select_fusion.1
  23.6 0.0 copy-start.1
  23.7 0.2 subtract_convert_fusion
  23.9 0.7 copy-done.1
  24.6 0.7 fusion.5
  25.3 0.4 fusion.31
  25.6 4.0 %convolution_convert_fusion.1 = bf16[64,16,512]{2,1,0:T(8,128)(2,1)S(1)} fusion(bf16[64,64,512]{2,1,0:T(8,128)(2,1)} %broadcast_select_fusion, f32[64,16]{1,0:T(8,128)S(1)} %fusion.31, f32[64,16,64]{2,1,0:T(8,128)S(1)} %fusion.5), kind=kOutput, calls=%fused_computation.5 | convolution fusion | flops 67830848 | bytes 5509120 | tf_op jit(solution)/shard_map/bhs,bsc->bhc/dot_general | solution.py:56
  29.7 2.9 %fusion.7 = bf16[16,8,8,128]{3,2,1,0:T(8,128)(2,1)S(1)} fusion(bf16[16,512,128]{2,1,0:T(8,128)(2,1)} %param.28, bf16[64,16,512]{2,1,0:T(8,128)(2,1)S(1)} %convolution_convert_fusion.1), kind=kOutput, calls=%fused_computation.14 | convolution fusion | flops 134348800 | bytes 3407872 | tf_op jit(solution)/shard_map/bhc,hcv->bhv/dot_general | solution.py:57
  32.6 5.1 %fusion.12 = (f32[64]{0:T(128)S(1)}, bf16[64,2048]{1,0:T(8,128)(2,1)S(1)}) fusion(bf16[2048,2048]{1,0:T(8,128)(2,1)} %param.29, bf16[16,8,8,128]{3,2,1,0:T(8,128)(2,1)S(1)} %fusion.7, bf16[64,2048]{1,0:T(8,128)(2,1)S(1)} %copy-done), kind=kOutput, calls=%fused_computation.25 | convolution fusion | flops 537657280 | bytes 9175296 | tf_op jit(solution)/shard_map/dot_general | solution.py:58
  37.8 0.7 copy-done.2
  38.5 0.1 fusion.14
  38.6 0.7 fusion.18.hx_ref
  39.3 0.3 copy.31
  39.6 0.9 pad.9.rtr_ref
  40.5 100.0 %moe.1 = bf16[64,2048]{1,0:T(8,128)(2,1)} custom-call(bf16[64,2176]{1,0:T(8,128)(2,1)} %fusion.18.hx_ref, bf16[64,2048]{1,0:T(8,128)(2,1)} %copy-done.2, bf16[2048,128]{1,0:T(8,128)(2,1)} %pad.9.rtr_ref, bf16[2048,2816]{1,0:T(8,128)(2,1)} %sg_hbm.1, bf16[2048,2816]{1,0:T(8,128)(2,1)} %su_hbm.1, bf16[2,1408,2048]{2,1,0:T(8,128)(2,1)} %bitcast.21, ...), custom_call_target="tpu_custom_call" | custom-call | tf_op jit(solution)/shard_map/moe/pallas_call | solution.py:405
  140.5 1.7 %copy.47 = bf16[64,2048]{1,0:T(8,128)(2,1)} copy(bf16[64,2048]{1,0:T(8,128)(2,1)} %moe.1) | data formatting | bytes 524288
  (21 shorter events, 0.2 us)
Async XLA Ops:
  6.9 4.0 %copy-start = (bf16[64,2048]{1,0:T(8,128)(2,1)S(1)}, bf16[64,2048]{1,0:T(8,128)(2,1)}, u32[]{:S(2)}) copy-start(bf16[64,2048]{1,0:T(8,128)(2,1)} %param.19) | copy-start | bytes 786436
  10.9 7.8 %copy-start.3 = (bf16[16,128,512]{2,1,0:T(8,128)(2,1)S(1)}, bf16[16,128,512]{2,1,0:T(8,128)(2,1)}, u32[]{:S(2)}) copy-start(bf16[16,128,512]{2,1,0:T(8,128)(2,1)} %param.27) | copy-start | bytes 6291460
  18.7 3.9 %copy-start.7 = (s32[64]{0:T(128)S(1)}, s32[64]{0:T(128)}, u32[]{:S(2)}) copy-start(s32[64]{0:T(128)} %param.22) | copy-start | bytes 772
  18.7 4.2 %copy-start.4 = (bf16[64,64,64]{2,1,0:T(8,128)(2,1)S(1)}, bf16[64,64,64]{2,1,0:T(8,128)(2,1)}, u32[]{:S(2)}) copy-start(bf16[64,64,64]{2,1,0:T(8,128)(2,1)} %param.21) | copy-start | bytes 1572868
  23.6 1.0 copy-start.1
  32.6 5.2 %copy-start.6 = (bf16[2048]{0:T(1024)(128)(2,1)S(1)}, bf16[2048]{0:T(1024)(128)(2,1)}, u32[]{:S(2)}) copy-start(bf16[2048]{0:T(1024)(128)(2,1)} %param.30) | copy-start | bytes 12292
  32.6 6.7 %copy-start.5 = (bf16[2048,64]{0,1:T(8,128)(2,1)S(1)}, bf16[2048,64]{0,1:T(8,128)(2,1)}, u32[]{:S(2)}) copy-start(bf16[2048,64]{0,1:T(8,128)(2,1)} %param.31) | copy-start | bytes 786436
  37.8 0.7 copy-start.2

commit v2 on v1

v2 whole, which is shorter than its diff:
```python
import jax
import jax.numpy as jnp
import numpy as np
from jax import lax
from jax.experimental import pallas as pl
from jax.experimental.pallas import tpu as pltpu
from jax.sharding import PartitionSpec as P

ROUTE_SCALE = 2.827
ROPE_BASE = 10000.0
NORM_EPS = 1e-6

MESH = pl.DeviceIdType.MESH
NE = 4
CAP = 12
SRC = 4
GRP = SRC * CAP
NCH = 8
CHUNKS = ((0, 1), (1, 1), (2, 2), (4, 2), (6, 2), (8, 2), (10, 2), (12, 2), (14, 1), (15, 1))
NA = 6
NB = 2
WIDE = 512
NP = 4
AHEAD = 2
TG = 16


def attn_kernel(pos_sm, x_ref, posr_ref, ids_ref, freq_ref, ag_ref, fg_ref, lat_hbm, rope_hbm, wq_hbm, wkv_hbm, wuk_hbm, wuv_hbm, wo_hbm,
                hx_ref, res_ref, lato_hbm, ropeo_hbm,
                lat, rope, wq, wkv, wuk, wuv, wo, abuf, latn, ropen, qlat, qrope, olat, ohead, posb, q_sem, m_sem):
    f32, bf16 = jnp.float32, jnp.bfloat16
    rows, dm = x_ref.shape
    heads, nope, rank = wuk.shape
    rd = rope.shape[2]
    seq = lat.shape[1]
    pairs = heads // 2
    pw = 2 * (nope + rd)

    def dot(a, b):
        return jnp.dot(a, b, preferred_element_type=f32)

    def q_copy(i):
        return pltpu.make_async_copy(wq_hbm.at[:, pl.ds(i * pw, pw)], wq.at[i], q_sem.at[i])

    def m_copy(i):
        src, dst = ((wkv_hbm, wkv), (wuk_hbm, wuk), (lat_hbm, lat), (rope_hbm, rope), (wuv_hbm, wuv), (wo_hbm, wo), (lat, lato_hbm), (rope, ropeo_hbm))[i]
        return pltpu.make_async_copy(src, dst, m_sem.at[i])

    m_copy(0).start()
    q_copy(0).start()
    q_copy(1).start()

    x = x_ref[...].astype(f32)
    scale = lax.rsqrt(jnp.mean(jnp.square(x), axis=-1, keepdims=True) + NORM_EPS)
    abuf[...] = (x * scale * ag_ref[...].astype(f32)[None, :]).astype(bf16)

    def dot_nt(a, b):
        return lax.dot_general(a, b, (((1,), (1,)), ((), ())), preferred_element_type=f32)

    def iota(shape, axis):
        return lax.broadcasted_iota(jnp.int32, shape, axis)

    eye = (iota((rows, rows), 0) == iota((rows, rows), 1)).astype(f32).astype(bf16)
    tri = (iota((rows, rows), 0) <= iota((rows, rows), 1)).astype(f32).astype(bf16)
    expert = iota((128, rows), 0)
    per_tok = jnp.zeros((128, rows), f32)
    for k in range(ids_ref.shape[0]):
        per_tok = per_tok + jnp.where(ids_ref[k:k + 1] == expert, 1.0, 0.0)
    code = (per_tok * dot(per_tok.astype(bf16), tri)).astype(bf16)
    hx_ref[:, :128] = dot_nt(eye, code).astype(bf16)
    posb[...] = dot_nt(eye, jnp.broadcast_to(posr_ref[...].astype(f32), (128, rows)).astype(bf16))
    angle = posb[...] * freq_ref[...]
    cos, sin = jnp.cos(angle), jnp.sin(angle)

    m_copy(0).wait()
    m_copy(1).start()
    for i in range(2, pairs):
        q_copy(i).start()
    for i in range(2, 6):
        m_copy(i).start()
    kv = dot_nt(abuf[...], wkv[pl.ds(0, rank)])
    latn[...] = (kv * lax.rsqrt(jnp.mean(jnp.square(kv), axis=-1, keepdims=True) + NORM_EPS)).astype(bf16).astype(f32)
    kr = dot_nt(abuf[...], wkv[pl.ds(rank, rd)])
    swapped = jnp.concatenate([-kr[:, rd // 2:], kr[:, :rd // 2]], axis=1)
    ropen[...] = (kr * cos[:, :rd] + swapped * sin[:, :rd]).astype(bf16).astype(f32)

    lo_half = lax.broadcasted_iota(jnp.int32, (1, 128), 1) < 64
    lo_quarter = lax.broadcasted_iota(jnp.int32, (1, 128), 1) < rd // 2

    def turn(v):
        swapped = jnp.where(lo_quarter, -pltpu.roll(v, 128 - rd // 2, 1), pltpu.roll(v, rd // 2, 1))
        return (v * cos + swapped * sin).astype(bf16)

    m_copy(1).wait()
    for i in range(pairs):
        q_copy(i).wait()
        qp = dot(abuf[...], wq[i]).astype(bf16)
        t1 = qp[:, 128:256].astype(f32)
        t2 = pltpu.roll(qp[:, 256:].astype(f32), 64, 1)
        odd = jnp.where(lo_half, pltpu.roll(t1, 64, 1), t2).astype(bf16)
        qlat[2 * i] = dot(qp[:, :128], wuk[2 * i]).astype(bf16)
        qlat[2 * i + 1] = dot(odd, wuk[2 * i + 1]).astype(bf16)
        qrope[2 * i] = turn(t1)
        qrope[2 * i + 1] = turn(t2)

    m_copy(2).wait()
    m_copy(3).wait()
    it16 = lax.broadcasted_iota(jnp.int32, (16, 1), 0)

    def update(t, carry):
        p = pos_sm[t]
        base = pl.multiple_of((p // 16) * 16, 16)
        hit = it16 == p - base
        lat[t, pl.ds(base, 16)] = jnp.where(hit, latn[pl.ds(t, 1)], lat[t, pl.ds(base, 16)].astype(f32)).astype(bf16)
        rope[t, pl.ds(base, 16)] = jnp.where(hit, ropen[pl.ds(t, 1)], rope[t, pl.ds(base, 16)].astype(f32)).astype(bf16)
        return carry
    lax.fori_loop(0, rows, update, 0, unroll=8)
    nk = TG * seq
    col = lax.broadcasted_iota(jnp.int32, (1, nk), 1)
    tok = lax.broadcasted_iota(jnp.int32, (TG, 1), 0)
    own = (col // seq) == tok
    col_j = col % seq

    for g in range(rows // TG):
        span = pl.ds(g * TG, TG)
        keys = lat[span].reshape(nk, rank)
        rkeys = rope[span].reshape(nk, rd)
        qg = qlat[:, span].reshape(heads * TG, rank)
        qr = qrope[:, span, pl.ds(0, rd)].reshape(heads * TG, rd)
        sc = dot_nt(qg, keys)
        sc = sc + dot_nt(qr, rkeys)
        sc = (sc * (nope + rd) ** -0.5).reshape(heads, TG, nk)
        seen = own & (col_j <= posb[span, pl.ds(0, 1)].astype(jnp.int32))
        sc = jnp.where(seen[None], sc, -jnp.inf)
        e = jnp.exp(sc - jnp.max(sc, axis=-1, keepdims=True))
        prob = (e / jnp.sum(e, axis=-1, keepdims=True)).astype(bf16).reshape(heads * TG, nk)
        olat[:, span] = dot(prob, keys).astype(bf16).reshape(heads, TG, rank)
        if g == 0:
            m_copy(6).start()
            m_copy(7).start()

    m_copy(4).wait()
    for h in range(heads):
        ohead[:, h * nope:(h + 1) * nope] = dot(olat[h], wuv[h]).astype(bf16)
    m_copy(5).wait()

    def out_tile(n, tot):
        cols = pl.ds(pl.multiple_of(n * 512, 512), 512)
        r = (x_ref[:, cols].astype(f32) + dot(ohead[...], wo[:, cols])).astype(bf16)
        res_ref[:, cols] = r
        rw = r.astype(f32)
        return tot + jnp.sum(rw * rw, axis=1, keepdims=True)
    tot = lax.fori_loop(0, dm // 512, out_tile, jnp.zeros((rows, 1), f32))
    scale = lax.rsqrt(tot / dm + NORM_EPS)
    hx_ref[:, 128:] = (res_ref[...].astype(f32) * scale * fg_ref[...].astype(f32)[None, :]).astype(bf16)
    m_copy(6).wait()
    m_copy(7).wait()


def attn_call(tok_in, lat_cache, rope_cache, tok_pos, expert_ids, attn_gain, w_query, w_kvdown, w_ukey, w_uval, w_out, ffn_gain):
    rows, dm = tok_in.shape
    heads, nope, rank = w_ukey.shape
    seq, rd = rope_cache.shape[1:]
    bf16, f32 = jnp.bfloat16, jnp.float32
    freq = ROPE_BASE ** (-(2.0 * np.arange(rd // 2)) / rd)
    freq = np.tile(freq.astype(np.float32), 128 // (rd // 2))[None, :]
    vm = pl.BlockSpec(memory_space=pltpu.VMEM)
    hb = pl.BlockSpec(memory_space=pl.ANY)
    pw = 2 * (nope + rd)
    return pl.pallas_call(
        attn_kernel,
        out_shape=(
            jax.ShapeDtypeStruct((rows, dm + 128), bf16),
            jax.ShapeDtypeStruct((rows, dm), bf16),
            jax.ShapeDtypeStruct(lat_cache.shape, bf16),
            jax.ShapeDtypeStruct(rope_cache.shape, bf16),
        ),
        in_specs=[pl.BlockSpec(memory_space=pltpu.SMEM)] + [vm] * 6 + [hb] * 7,
        out_specs=(vm, vm, hb, hb),
        scratch_shapes=[
            pltpu.VMEM(lat_cache.shape, bf16),
            pltpu.VMEM(rope_cache.shape, bf16),
            pltpu.VMEM((heads // 2, dm, pw), bf16),
            pltpu.VMEM(w_kvdown.shape[::-1], bf16),
            pltpu.VMEM(w_ukey.shape, bf16),
            pltpu.VMEM(w_uval.shape, bf16),
            pltpu.VMEM(w_out.shape, bf16),
            pltpu.VMEM((rows, dm), bf16),
            pltpu.VMEM((rows, rank), f32),
            pltpu.VMEM((rows, rd), f32),
            pltpu.VMEM((heads, rows, rank), bf16),
            pltpu.VMEM((heads, rows, 128), bf16),
            pltpu.VMEM((heads, rows, rank), bf16),
            pltpu.VMEM((rows, heads * nope), bf16),
            pltpu.VMEM((rows, 128), f32),
            pltpu.SemaphoreType.DMA((heads // 2,)),
            pltpu.SemaphoreType.DMA((8,)),
        ],
        compiler_params=pltpu.CompilerParams(vmem_limit_bytes=60 * 1024 * 1024),
        name="attn",
    )(tok_pos, tok_in, tok_pos[None, :], expert_ids.T, jnp.asarray(freq), attn_gain, ffn_gain,
      lat_cache, rope_cache, w_query, w_kvdown.T, w_ukey, w_uval, w_out)


def moe_kernel(hx_ref, res_ref, rtr_ref, sg_hbm, su_hbm, sd_hbm, eg_hbm, eu_hbm, ed_hbm, out_ref,
               hall, xbuf, act, sact, sout, abuf, bbuf, sbuf, rbuf, fbuf, zbuf, rly, w3, pick,
               a_sem, b_sem, zup_s, zdn_s, z_r, y_s, y_r, c_s, c_r, s_s, s_r, f_s, f_r, l_s, l_r):
    f32, bf16 = jnp.float32, jnp.bfloat16
    dm = res_ref.shape[1]
    rows = res_ref.shape[0]
    ff = act.shape[2]
    cw = dm // NCH
    me = lax.axis_index("ep")
    z, q = me // 4, me % 4
    qy = jnp.where(q >= 2, q - 2, q + 2)
    qc = jnp.where(q % 2 == 1, q - 1, q + 1)
    qd = 3 - q
    peers = (qc, qy, qd)

    def dev(zz, qq):
        return {"ep": zz * 4 + qq}

    def a_src(u):
        if u < 4:
            return (sg_hbm, su_hbm)[u % 2].at[:, pl.ds((u // 2) * ff, ff)]
        return (eg_hbm, eu_hbm)[u % 2].at[(u - 4) // 2]

    def a_copy(u):
        return pltpu.make_async_copy(a_src(u), abuf.at[u % NA], a_sem.at[u % NA])

    def sd_copy(p, hf):
        return pltpu.make_async_copy(sd_hbm.at[:, :, pl.ds((2 * p + hf) * cw, cw)], bbuf.at[p % NB, pl.ds(2 * hf, 2)], b_sem.at[p % NB, hf])

    def b_copy(cc):
        return pltpu.make_async_copy(ed_hbm.at[:, :, pl.ds(cc * cw, cw)], bbuf.at[cc % NB], b_sem.at[cc % NB, 0])

    for u in range(2):
        a_copy(u).start()

    bar = pltpu.get_barrier_semaphore()
    for s in range(1, 4):
        pl.semaphore_signal(bar, inc=1, device_id=dev((z + s) % 4, q), device_id_type=MESH)
    for qq in peers:
        pl.semaphore_signal(bar, inc=1, device_id=dev(z, qq), device_id_type=MESH)
    pl.semaphore_wait(bar, 6)

    def rcopy(src, dst, ss, rs, d):
        return pltpu.make_async_remote_copy(src_ref=src, dst_ref=dst, send_sem=ss, recv_sem=rs, device_id=d, device_id_type=MESH)

    cut = [0] + [128 + dm * k // NP for k in range(1, NP + 1)]

    def part(ref, p):
        return ref.at[:, pl.ds(cut[p], cut[p + 1] - cut[p])]

    def blk(qq, b, p):
        return part(hall.at[qq, b], p)

    def up(src, b, p):
        return rcopy(src, blk(q, b, p), zup_s.at[b, p], z_r.at[b, p], dev(z + 1, q))

    def dn(src, b, p):
        return rcopy(src, blk(q, b, p), zdn_s.at[b, p], z_r.at[b, p], dev(z - 1, q))

    def ysend(src, b, p):
        return rcopy(src, blk(q, b, p), y_s.at[b, p], y_r.at[b, p], dev(z, qy))

    def yrecv(b, p):
        return rcopy(blk(qy, b, p), blk(qy, b, p), y_s.at[b, p], y_r.at[b, p], dev(z, qy))

    def csend(src, qq, k, b, p):
        return rcopy(src, blk(qq, b, p), c_s.at[k, b, p], c_r.at[k, b, p], dev(z, qc))

    for p in range(NP):
        mine = part(hx_ref, p)

        @pl.when(z < 3)
        def _():
            up(mine, z, p).start()

        @pl.when(z > 0)
        def _():
            dn(mine, z, p).start()

        ysend(mine, z, p).start()
    for p in range(NP):
        csend(part(hx_ref, p), q, 0, z, p).start()
    for u in range(2, 4):
        a_copy(u).start()
    hall[q, z] = hx_ref[...]

    def gather_step(s, p):
        if s <= 3:
            @pl.when(z - s >= 0)
            def _():
                b = z - s
                src = blk(q, b, p)
                up(src, b, p).wait_recv()

                @pl.when(z < 3)
                def _():
                    up(src, b, p).start()
                ysend(src, b, p).start()
                csend(src, q, 0, b, p).start()

            @pl.when(z + s <= 3)
            def _():
                b = z + s
                src = blk(q, b, p)
                dn(src, b, p).wait_recv()

                @pl.when(z > 0)
                def _():
                    dn(src, b, p).start()
                ysend(src, b, p).start()
                csend(src, q, 0, b, p).start()
        t = s - 1
        for sign in ((1, -1) if t else (1,)):
            b = z - sign * t

            @pl.when((b >= 0) & (b <= 3))
            def _():
                yrecv(b, p).wait_recv()
                csend(blk(qy, b, p), qy, 1, b, p).start()

    def dot(a, b):
        return jnp.dot(a, b, preferred_element_type=f32)

    def gate_up(x, sg, su, store, lo, hi):
        off = lo
        while off < hi:
            width = min(WIDE, hi - off)
            g = dot(x(), abuf[sg, :, pl.ds(off, width)])
            u = dot(x(), abuf[su, :, pl.ds(off, width)])
            store(off, width, (g * jax.nn.sigmoid(g) * u).astype(bf16))
            off += width

    def sh_put(j):
        def put(off, width, v):
            sact[j, :, pl.ds(off, width)] = v
        return put

    def sh_gate_up(j, part):
        cols = (0, ff // 256 // 2 * 256, ff)
        if part == 0:
            a_copy(2 * j).wait()
            a_copy(2 * j + 1).wait()
        gate_up(lambda: hx_ref[:, pl.ds(128, dm)], (2 * j) % NA, (2 * j + 1) % NA, sh_put(j), cols[part], cols[part + 1])

    def sh_down(p):
        for hf in range(2):
            sd_copy(p, hf).wait()
            sout[2 * p + hf] = dot(sact[0], bbuf[p % NB, 2 * hf]) + dot(sact[1], bbuf[p % NB, 2 * hf + 1])
        if p + NB < NCH // 2:
            for hf in range(2):
                sd_copy(p + NB, hf).start()
        else:
            b_copy(p + NB - NCH // 2).start()

    sh_gate_up(0, 0)
    sh_gate_up(0, 1)
    for p in range(NB):
        for hf in range(2):
            sd_copy(p, hf).start()
    gather_step(1, 0)
    gather_step(1, 1)
    sh_gate_up(1, 0)
    gather_step(1, 2)
    sh_gate_up(1, 1)
    gather_step(1, 3)
    sh_down(0)
    gather_step(2, 0)
    sh_down(1)
    for u in range(4, 4 + NA):
        a_copy(u).start()
    gather_step(2, 1)
    sh_down(2)
    gather_step(2, 2)
    sh_down(3)
    gather_step(2, 3)

    def spread():
        ee = lax.broadcasted_iota(jnp.int32, (rtr_ref.shape[0], SRC * NE * GRP), 0)
        col = lax.broadcasted_iota(jnp.int32, (1, SRC * NE * GRP), 1)
        col48 = lax.rem(col, GRP)
        col_z = lax.div(col48, CAP)
        col_k = (lax.rem(col48, CAP) + 1).astype(f32)
        blk = lax.div(col, NE * GRP)
        owner = jnp.where(blk == 0, q, jnp.where(blk == 1, qc, jnp.where(blk == 2, qy, qd)))
        rep = (ee == SRC * NE * z + NE * owner + lax.div(lax.rem(col, NE * GRP), GRP)).astype(f32).astype(bf16)
        for b in range(SRC):
            hz = hall[q, b, :, pl.ds(128, dm)]
            code = hall[q, b, :, pl.ds(0, rtr_ref.shape[0])]
            s = jax.nn.sigmoid(lax.dot_general(hz, rtr_ref[...], (((1,), (1,)), ((), ())), preferred_element_type=f32))
            chosen = jnp.where(code.astype(f32) > 0.0, s, 0.0)
            w = ROUTE_SCALE * chosen / jnp.sum(chosen, axis=1, keepdims=True)
            hi = w.astype(bf16)
            r1 = w - hi.astype(f32)
            mid = r1.astype(bf16)
            low = (r1 - mid.astype(f32)).astype(bf16)
            ok = (dot(code, rep) == col_k) & (col_z == b)
            for i, part in enumerate((hi, mid, low)):
                w3[i, pl.ds(b * rows, rows)] = jnp.where(ok, dot(part, rep), 0.0).astype(bf16)

    def find(g):
        nr = NE * GRP
        ee = lax.broadcasted_iota(jnp.int32, (nr, 128), 1)
        ri = lax.broadcasted_iota(jnp.int32, (nr, 128), 0)
        lo = (ee - NE * me) * GRP
        sel = ((ri >= lo) & (ri < lo + GRP)).astype(f32).astype(bf16)
        rcol = lax.broadcasted_iota(jnp.int32, (nr, 1), 0)
        r48 = lax.rem(rcol, GRP)
        row_z = lax.div(r48, CAP)
        row_k = (lax.rem(r48, CAP) + 1).astype(f32)
        code = hall[g, :, :, pl.ds(0, 128)].reshape(SRC * rows, 128)
        ct = lax.dot_general(sel, code, (((1,), (1,)), ((), ())), preferred_element_type=f32)
        tz = lax.div(lax.broadcasted_iota(jnp.int32, (1, SRC * rows), 1), rows)
        pick[g] = jnp.where((ct == row_k) & (row_z == tz), 1.0, 0.0).astype(bf16)

    def select(g, p):
        wide = dm // NP
        hz = hall[g, :, :, pl.ds(128 + p * wide, wide)].reshape(SRC * rows, wide)
        x = dot(pick[g], hz).astype(bf16)
        for i in range(NE):
            xbuf[i, g, :, pl.ds(p * wide, wide)] = x[i * GRP:(i + 1) * GRP]

    for p in range(NP):
        gather_step(3, p)
        if p == 0:
            find(q)
        select(q, p)
    for p in range(NP):
        gather_step(4, p)
        for k, qq in ((0, qc), (1, qd)):
            for b in range(SRC):
                rcopy(blk(qq, b, p), blk(qq, b, p), c_s.at[k, b, p], c_r.at[k, b, p], dev(z, qc)).wait_recv()
        for qq in peers:
            if p == 0:
                find(qq)
            select(qq, p)

    def expert(i, carry):
        slot = lax.rem(2 * i + 4, NA)
        for w, src in enumerate((eg_hbm, eu_hbm)):
            pltpu.make_async_copy(src.at[i], abuf.at[slot + w], a_sem.at[slot + w]).wait()

        def put(off, width, v):
            act[i, :, pl.ds(off, width)] = v
        gate_up(lambda: xbuf[i].reshape(SRC * GRP, dm), slot, slot + 1, put, 0, ff)

        @pl.when(i + NA // 2 < NE)
        def _():
            for w, src in enumerate((eg_hbm, eu_hbm)):
                pltpu.make_async_copy(src.at[i + NA // 2], abuf.at[slot + w], a_sem.at[slot + w]).start()
        return carry
    lax.fori_loop(0, NE, expert, 0)

    def s_copy(cc, j):
        g0, n = CHUNKS[cc]
        return rcopy(sbuf.at[pl.ds(g0, n), peers[j]], rbuf.at[pl.ds(g0, n), j], s_s.at[cc, j], s_r.at[cc, j], dev(z, peers[j]))

    def down(cc):
        g0, n = CHUNKS[cc]
        w = g0 * 128 // cw
        off = g0 * 128 % cw
        if off == 0:
            b_copy(w).wait()
        for i in range(NE):
            o = dot(act[i], bbuf[w % NB, i, :, pl.ds(off, n * 128)]).astype(bf16)
            for g in range(4):
                for t in range(n):
                    sbuf[g0 + t, g, pl.ds(i * GRP, GRP)] = o[g * GRP:(g + 1) * GRP, t * 128:(t + 1) * 128]
        for j in (2, 1, 0):
            s_copy(cc, j).start()
        if off + n * 128 == cw and w + NB < NCH:
            b_copy(w + NB).start()

    edge = (z == 0) | (z == 3)
    z_edge = jnp.where(z <= 1, 0, 3)
    z_mid = jnp.where(z <= 1, 1, 2)
    z_mid2 = 3 - z_mid
    z_edge2 = 3 - z_edge

    def f_copy(cc, dst_z, k, rk):
        g0, n = CHUNKS[cc]
        return rcopy(fbuf.at[pl.ds(g0, n), dst_z], zbuf.at[pl.ds(g0, n), rk], f_s.at[cc, k], f_r.at[cc, rk], dev(dst_z, q))

    def l_copy(cc):
        g0, n = CHUNKS[cc]
        return rcopy(fbuf.at[pl.ds(g0, n), z_edge2], rly.at[pl.ds(g0, n)], l_s.at[cc], l_r.at[cc], dev(z_mid, q))

    def combine(cc):
        g0, n = CHUNKS[cc]
        for j in range(3):
            s_copy(cc, j).wait_recv()
        got = jnp.concatenate([jnp.concatenate([sbuf[g0 + t, q]] + [rbuf[g0 + t, j] for j in range(3)], axis=0) for t in range(n)], axis=1)
        acc = dot(w3[0], got) + (dot(w3[1], got) + dot(w3[2], got))
        for t in range(n):
            fbuf[g0 + t] = acc[:, t * 128:(t + 1) * 128].reshape(SRC, rows, 128)

        @pl.when(edge)
        def _():
            l_copy(cc).start()
            f_copy(cc, z_mid2, 1, 2).start()
            f_copy(cc, z_mid, 0, 0).start()

        @pl.when(jnp.logical_not(edge))
        def _():
            f_copy(cc, z_mid2, 1, 1).start()
            f_copy(cc, z_edge, 0, 0).start()

    def relay(cc):
        g0, n = CHUNKS[cc]

        @pl.when(jnp.logical_not(edge))
        def _():
            l_copy(cc).wait_recv()
            for t in range(g0, g0 + n):
                fbuf[t, z_edge2] += rly[t]
            f_copy(cc, z_edge2, 2, 1).start()

    def final(cc):
        g0, n = CHUNKS[cc]

        def finish(parts):
            for rk in range(parts):
                f_copy(cc, z_mid, 0, rk).wait_recv()
            for t in range(g0, g0 + n):
                cols = pl.ds(t * 128, 128)
                tot = fbuf[t, z]
                for rk in range(parts):
                    tot = tot + zbuf[t, rk]
                sh = sout[t * 128 // cw, :, pl.ds(t * 128 % cw, 128)]
                out_ref[:, cols] = (res_ref[:, cols].astype(f32) + sh + tot).astype(bf16)

        @pl.when(edge)
        def _():
            finish(2)

        @pl.when(jnp.logical_not(edge))
        def _():
            finish(3)

    last = len(CHUNKS) - 1
    for cc in range(AHEAD):
        down(cc)
    spread()
    for cc in range(last + 1):
        if cc + AHEAD <= last:
            down(cc + AHEAD)
        combine(cc)
        if cc:
            relay(cc - 1)
    relay(last)
    for cc in range(last + 1):
        final(cc)

    for p in range(NP):
        @pl.when(z < 3)
        def _():
            up(part(hx_ref, p), z, p).wait_send()

        @pl.when(z > 0)
        def _():
            dn(part(hx_ref, p), z, p).wait_send()

        for s in range(1, 4):
            @pl.when((z - s >= 0) & (z < 3))
            def _():
                up(blk(q, z - s, p), z - s, p).wait_send()

            @pl.when((z + s <= 3) & (z > 0))
            def _():
                dn(blk(q, z + s, p), z + s, p).wait_send()
        for b in range(SRC):
            ysend(blk(q, b, p), b, p).wait_send()
            csend(blk(q, b, p), q, 0, b, p).wait_send()
            csend(blk(qy, b, p), qy, 1, b, p).wait_send()
    for cc in range(last + 1):
        for j in range(3):
            s_copy(cc, j).wait_send()
        f_copy(cc, z_mid, 0, 0).wait_send()
        f_copy(cc, z_mid, 1, 0).wait_send()

        @pl.when(edge)
        def _():
            l_copy(cc).wait_send()

        @pl.when(jnp.logical_not(edge))
        def _():
            f_copy(cc, z_edge2, 2, 1).wait_send()


def moe_call(hx, resid, router, sh_gate, sh_up, sh_down, ex_gate, ex_up, ex_down):
    rows, dm = resid.shape
    ff = ex_gate.shape[2]
    cw = dm // NCH
    bf16, f32 = jnp.bfloat16, jnp.float32
    vm = pl.BlockSpec(memory_space=pltpu.VMEM)
    hb = pl.BlockSpec(memory_space=pl.ANY)
    sem = pltpu.SemaphoreType.DMA
    nk = NE * GRP
    return pl.pallas_call(
        moe_kernel,
        out_shape=jax.ShapeDtypeStruct((rows, dm), bf16),
        in_specs=[vm] * 3 + [hb] * 6,
        out_specs=vm,
        scratch_shapes=[
            pltpu.VMEM((4, SRC, rows, dm + 128), bf16),
            pltpu.VMEM((NE, 4, GRP, dm), bf16),
            pltpu.VMEM((NE, SRC * GRP, ff), bf16),
            pltpu.VMEM((2, rows, ff), bf16),
            pltpu.VMEM((NCH, rows, cw), f32),
            pltpu.VMEM((NA, dm, ff), bf16),
            pltpu.VMEM((NB, NE, ff, cw), bf16),
            pltpu.VMEM((dm // 128, 4, nk, 128), bf16),
            pltpu.VMEM((dm // 128, 3, nk, 128), bf16),
            pltpu.VMEM((dm // 128, SRC, rows, 128), f32),
            pltpu.VMEM((dm // 128, 3, rows, 128), f32),
            pltpu.VMEM((dm // 128, rows, 128), f32),
            pltpu.VMEM((3, SRC * rows, SRC * nk), bf16),
            pltpu.VMEM((4, nk, SRC * rows), bf16),
            sem((NA,)), sem((NB, 2)),
            sem((4, NP)), sem((4, NP)), sem((4, NP)),
            sem((4, NP)), sem((4, NP)),
            sem((2, 4, NP)), sem((2, 4, NP)),
            sem((len(CHUNKS), 3)), sem((len(CHUNKS), 3)),
            sem((len(CHUNKS), 3)), sem((len(CHUNKS), 3)),
            sem((len(CHUNKS),)), sem((len(CHUNKS),)),
        ],
        compiler_params=pltpu.CompilerParams(collective_id=0, has_side_effects=True, vmem_limit_bytes=66 * 1024 * 1024 - 2 * 1024 * 1024 - 65536),
        name="moe",
    )(hx, resid, router.T, sh_gate, sh_up, sh_down.reshape(2, ff, dm), ex_gate, ex_up, ex_down)


def solution(mesh):
    row_one = P(('dp', 'ep'))
    row_two = P(('dp', 'ep'), None)
    row_three = P(('dp', 'ep'), None, None)
    rep_one = P(None)
    rep_two = P(None, None)
    rep_three = P(None, None, None)
    exp_spec = P('ep', None, None)

    def local_step(tok_in, lat_cache, rope_cache, tok_pos, expert_ids, attn_gain, w_query, w_kvdown, w_ukey, w_uval, w_out, ffn_gain, w_router, sh_gate, sh_up, sh_down, ex_gate, ex_up, ex_down):
        hx, resid, lat_out, rope_out = attn_call(tok_in, lat_cache, rope_cache, tok_pos, expert_ids, attn_gain, w_query, w_kvdown, w_ukey, w_uval, w_out, ffn_gain)
        out_hidden = moe_call(hx, resid, w_router, sh_gate, sh_up, sh_down, ex_gate, ex_up, ex_down)
        return out_hidden, lat_out, rope_out

    in_specs = (row_two, row_three, row_three, row_one, row_two, rep_one, rep_two, rep_two, rep_three, rep_three, rep_two, rep_one, rep_two, rep_two, rep_two, rep_two, exp_spec, exp_spec, exp_spec)
    out_specs = (row_two, row_three, row_three)
    return jax.shard_map(local_step, mesh=mesh, in_specs=in_specs, out_specs=out_specs, check_vma=False)
```

time: 143 us -> 119 us (0.83)
  matrix products: 26.3 us -> 0 us
  Pallas kernels: 100 us -> 117 us
  other arithmetic: 10.1 us -> 0 us
  local copies, waits for them, and re-layouts: 4.89 us -> 1.67 us
    dot_general x8 -> x0, matrix products: 26.3 us -> none  [the longest x1 7.09 us: attention_block(): jnp.dot(x_norm, w_query, preferred_element_type=jnp.float32)]
    pallas_call x0 -> x1, Pallas kernels: none -> 19 us  [attn_call(): pl.pallas_call(attn_kernel, out_shape=(jax.ShapeDtypeStruct((rows, dm + 1...]
    select_n x2 -> x0, other arithmetic: 4.71 us -> none  [the longest x1 3.99 us: attention_block(): lat_out = jnp.where(at_pos, lat_new[:, None, :], lat_cache)]
    pallas_call x1, Pallas kernels: 100 us -> 97.7 us  [moe_call(): pl.pallas_call(moe_kernel, out_shape=jax.ShapeDtypeStruct((rows, dm), bf1...]
    reduce_sum x3 -> x0, other arithmetic: 2.02 us -> none  [the longest x2 1.21 us: unit_norm(): mean_sq = jnp.mean(jnp.square(values), axis=-1, keepdims=True)]
    unnamed x18 -> x1, local copies, waits for them, and re-layouts: 3.34 us -> 1.67 us
where the time goes in v2:
time: 119 us
  Pallas kernels  117 us (98%)
  local copies, waits for them, and re-layouts  1.67 us (1%)
    pallas_call x1, Pallas kernels, moe_call(): pl.pallas_call(moe_kernel, out_shape=jax.ShapeDtypeStruct((rows, dm), bf1...  97.7 us
    pallas_call x1, Pallas kernels, attn_call(): pl.pallas_call(attn_kernel, out_shape=(jax.ShapeDtypeStruct((rows, dm + 1...  19 us

profile of v2, /device:TPU:0, one launch (start us, length us, event | category | flops | bytes accessed | tf_op | source)
XLA Modules:
  0.0 119.0 jit_solution(14982720682947045604)
XLA Ops:
  0.6 19.0 %attn.1 = (bf16[64,2176]{1,0:T(8,128)(2,1)}, bf16[64,2048]{1,0:T(8,128)(2,1)}, bf16[64,64,512]{2,1,0:T(8,128)(2,1)}, bf16[64,64,64]{2,1,0:T(8,128)(2,1)}) custom-call(s32[64]{0:T(128)} %pos_sm.1, bf16[64,2048]{1,0:T(8,128)(2,1)} %x_ref.1, s32[1,64]{1,0:T(1,128)} %bitcast.9, s32[6,64]{1,0:T(8,128)} %bitcast.8, f32[1,128]{1,0:T(1,128)} %constant.2.clone.freq_ref, ...), custom_call_target="tpu_custom_call" | custom-call | tf_op jit(solution)/shard_map/attn/pallas_call | solution.py:170
  19.6 97.7 %moe.1 = bf16[64,2048]{1,0:T(8,128)(2,1)} custom-call(bf16[64,2176]{1,0:T(8,128)(2,1)} %get-tuple-element.7.hx_ref, bf16[64,2048]{1,0:T(8,128)(2,1)} %get-tuple-element.8.res_ref, bf16[64,2048]{1,0:T(8,128)(2,1)} %bitcast.7, bf16[2048,2816]{1,0:T(8,128)(2,1)} %sg_hbm.1, bf16[2048,2816]{1,0:T(8,128)(2,1)} %su_hbm.1, bf16[2,1408,2048]{2,1,0:T(8,128)(2,1)} %bitcast.5, ...), custom_call_target="tpu_custom_call" | custom-call | tf_op jit(solution)/shard_map/moe/pallas_call | solution.py:602
  117.3 1.7 %copy.24 = bf16[64,2048]{1,0:T(8,128)(2,1)} copy(bf16[64,2048]{1,0:T(8,128)(2,1)} %moe.1) | data formatting | bytes 524288

commit v3 on v2

--- a/solution.py
+++ b/solution.py
@@ -47,6 +47,7 @@
         return pltpu.make_async_copy(src, dst, m_sem.at[i])
 
     m_copy(0).start()
+    m_copy(1).start()
     q_copy(0).start()
     q_copy(1).start()
 
@@ -73,7 +74,6 @@
     cos, sin = jnp.cos(angle), jnp.sin(angle)
 
     m_copy(0).wait()
-    m_copy(1).start()
     for i in range(2, pairs):
         q_copy(i).start()
     for i in range(2, 6):
@@ -144,13 +144,13 @@
         ohead[:, h * nope:(h + 1) * nope] = dot(olat[h], wuv[h]).astype(bf16)
     m_copy(5).wait()
 
-    def out_tile(n, tot):
-        cols = pl.ds(pl.multiple_of(n * 512, 512), 512)
+    tot = jnp.zeros((rows, 1), f32)
+    for n in range(dm // 512):
+        cols = pl.ds(n * 512, 512)
         r = (x_ref[:, cols].astype(f32) + dot(ohead[...], wo[:, cols])).astype(bf16)
         res_ref[:, cols] = r
         rw = r.astype(f32)
-        return tot + jnp.sum(rw * rw, axis=1, keepdims=True)
-    tot = lax.fori_loop(0, dm // 512, out_tile, jnp.zeros((rows, 1), f32))
+        tot = tot + jnp.sum(rw * rw, axis=1, keepdims=True)
     scale = lax.rsqrt(tot / dm + NORM_EPS)
     hx_ref[:, 128:] = (res_ref[...].astype(f32) * scale * fg_ref[...].astype(f32)[None, :]).astype(bf16)
     m_copy(6).wait()
@@ -204,7 +204,7 @@
 
 def moe_kernel(hx_ref, res_ref, rtr_ref, sg_hbm, su_hbm, sd_hbm, eg_hbm, eu_hbm, ed_hbm, out_ref,
                hall, xbuf, act, sact, sout, abuf, bbuf, sbuf, rbuf, fbuf, zbuf, rly, w3, pick,
-               a_sem, b_sem, zup_s, zdn_s, z_r, y_s, y_r, c_s, c_r, s_s, s_r, f_s, f_r, l_s, l_r):
+               a_sem, b_sem, zup_s, zdn_s, z_r, y_s, y_r, xu_s, xd_s, x_r, c_s, c_r, s_s, s_r, f_s, f_r, l_s, l_r):
     f32, bf16 = jnp.float32, jnp.bfloat16
     dm = res_ref.shape[1]
     rows = res_ref.shape[0]
@@ -217,6 +217,13 @@
     qd = 3 - q
     peers = (qc, qy, qd)
 
+    def fenced(f):
+        def run(*args):
+            @pl.when(me >= 0)
+            def _():
+                f(*args)
+        return run
+
     def dev(zz, qq):
         return {"ep": zz * 4 + qq}
 
@@ -288,7 +295,15 @@
         a_copy(u).start()
     hall[q, z] = hx_ref[...]
 
+    def xup(p):
+        return rcopy(blk(qy, 0, p), blk(qy, 0, p), xu_s.at[p], x_r.at[0, p], dev(z + 1, q))
+
+    def xdn(p):
+        return rcopy(blk(qy, 3, p), blk(qy, 3, p), xd_s.at[p], x_r.at[1, p], dev(z - 1, q))
+
+    @fenced
     def gather_step(s, p):
+        late = p >= NP // 2
         if s <= 3:
             @pl.when(z - s >= 0)
             def _():
@@ -299,7 +314,10 @@
                 @pl.when(z < 3)
                 def _():
                     up(src, b, p).start()
-                ysend(src, b, p).start()
+
+                @pl.when((b > 0) | (not late))
+                def _():
+                    ysend(src, b, p).start()
                 csend(src, q, 0, b, p).start()
 
             @pl.when(z + s <= 3)
@@ -311,16 +329,55 @@
                 @pl.when(z > 0)
                 def _():
                     dn(src, b, p).start()
-                ysend(src, b, p).start()
+
+                @pl.when((b < 3) | (not late))
+                def _():
+                    ysend(src, b, p).start()
                 csend(src, q, 0, b, p).start()
         t = s - 1
-        for sign in ((1, -1) if t else (1,)):
-            b = z - sign * t
-
-            @pl.when((b >= 0) & (b <= 3))
+        if t == 0:
+            yrecv(z, p).wait_recv()
+            csend(blk(qy, z, p), qy, 1, z, p).start()
+            if late:
+                @pl.when(z == 0)
+                def _():
+                    xup(p).start()
+
+                @pl.when(z == 3)
+                def _():
+                    xdn(p).start()
+            return
+
+        def over_y(b):
+            yrecv(b, p).wait_recv()
+            csend(blk(qy, b, p), qy, 1, b, p).start()
+
+        @pl.when((z - t > 0) if late else (z - t >= 0))
+        def _():
+            over_y(z - t)
+
+        @pl.when((z + t < 3) if late else (z + t <= 3))
+        def _():
+            over_y(z + t)
+
+        if late:
+            @pl.when(z == t)
             def _():
-                yrecv(b, p).wait_recv()
-                csend(blk(qy, b, p), qy, 1, b, p).start()
+                xup(p).wait_recv()
+
+                @pl.when(z < 3)
+                def _():
+                    xup(p).start()
+                csend(blk(qy, 0, p), qy, 1, 0, p).start()
+
+            @pl.when(z == 3 - t)
+            def _():
+                xdn(p).wait_recv()
+
+                @pl.when(z > 0)
+                def _():
+                    xdn(p).start()
+                csend(blk(qy, 3, p), qy, 1, 3, p).start()
 
     def dot(a, b):
         return jnp.dot(a, b, preferred_element_type=f32)
@@ -339,6 +396,7 @@
             sact[j, :, pl.ds(off, width)] = v
         return put
 
+    @fenced
     def sh_gate_up(j, part):
         cols = (0, ff // 256 // 2 * 256, ff)
         if part == 0:
@@ -346,6 +404,7 @@
             a_copy(2 * j + 1).wait()
         gate_up(lambda: hx_ref[:, pl.ds(128, dm)], (2 * j) % NA, (2 * j + 1) % NA, sh_put(j), cols[part], cols[part + 1])
 
+    @fenced
     def sh_down(p):
         for hf in range(2):
             sd_copy(p, hf).wait()
@@ -378,6 +437,7 @@
     sh_down(3)
     gather_step(2, 3)
 
+    @fenced
     def spread():
         ee = lax.broadcasted_iota(jnp.int32, (rtr_ref.shape[0], SRC * NE * GRP), 0)
         col = lax.broadcasted_iota(jnp.int32, (1, SRC * NE * GRP), 1)
@@ -401,6 +461,7 @@
             for i, part in enumerate((hi, mid, low)):
                 w3[i, pl.ds(b * rows, rows)] = jnp.where(ok, dot(part, rep), 0.0).astype(bf16)
 
+    @fenced
     def find(g):
         nr = NE * GRP
         ee = lax.broadcasted_iota(jnp.int32, (nr, 128), 1)
@@ -416,6 +477,7 @@
         tz = lax.div(lax.broadcasted_iota(jnp.int32, (1, SRC * rows), 1), rows)
         pick[g] = jnp.where((ct == row_k) & (row_z == tz), 1.0, 0.0).astype(bf16)
 
+    @fenced
     def select(g, p):
         wide = dm // NP
         hz = hall[g, :, :, pl.ds(128 + p * wide, wide)].reshape(SRC * rows, wide)
@@ -428,8 +490,10 @@
         if p == 0:
             find(q)
         select(q, p)
+    gather_step(4, 0)
     for p in range(NP):
-        gather_step(4, p)
+        if p + 1 < NP:
+            gather_step(4, p + 1)
         for k, qq in ((0, qc), (1, qd)):
             for b in range(SRC):
                 rcopy(blk(qq, b, p), blk(qq, b, p), c_s.at[k, b, p], c_r.at[k, b, p], dev(z, qc)).wait_recv()
@@ -458,6 +522,7 @@
         g0, n = CHUNKS[cc]
         return rcopy(sbuf.at[pl.ds(g0, n), peers[j]], rbuf.at[pl.ds(g0, n), j], s_s.at[cc, j], s_r.at[cc, j], dev(z, peers[j]))
 
+    @fenced
     def down(cc):
         g0, n = CHUNKS[cc]
         w = g0 * 128 // cw
@@ -474,6 +539,7 @@
         if off + n * 128 == cw and w + NB < NCH:
             b_copy(w + NB).start()
 
+    last = len(CHUNKS) - 1
     edge = (z == 0) | (z == 3)
     z_edge = jnp.where(z <= 1, 0, 3)
     z_mid = jnp.where(z <= 1, 1, 2)
@@ -488,6 +554,7 @@
         g0, n = CHUNKS[cc]
         return rcopy(fbuf.at[pl.ds(g0, n), z_edge2], rly.at[pl.ds(g0, n)], l_s.at[cc], l_r.at[cc], dev(z_mid, q))
 
+    @fenced
     def combine(cc):
         g0, n = CHUNKS[cc]
         for j in range(3):
@@ -500,14 +567,16 @@
         @pl.when(edge)
         def _():
             l_copy(cc).start()
-            f_copy(cc, z_mid2, 1, 2).start()
-            f_copy(cc, z_mid, 0, 0).start()
+            for c in ((cc - 1, cc) if cc == last else (cc,) if cc < last - 1 else ()):
+                f_copy(c, z_mid2, 1, 2).start()
+                f_copy(c, z_mid, 0, 0).start()
 
         @pl.when(jnp.logical_not(edge))
         def _():
             f_copy(cc, z_mid2, 1, 1).start()
             f_copy(cc, z_edge, 0, 0).start()
 
+    @fenced
     def relay(cc):
         g0, n = CHUNKS[cc]
 
@@ -518,6 +587,7 @@
                 fbuf[t, z_edge2] += rly[t]
             f_copy(cc, z_edge2, 2, 1).start()
 
+    @fenced
     def final(cc):
         g0, n = CHUNKS[cc]
 
@@ -540,7 +610,6 @@
         def _():
             finish(3)
 
-    last = len(CHUNKS) - 1
     for cc in range(AHEAD):
         down(cc)
     spread()
@@ -554,6 +623,18 @@
     for cc in range(last + 1):
         final(cc)
 
+    for p in range(NP // 2, NP):
+        @pl.when(z < 3)
+        def _():
+            xup(p).wait_send()
+
+        @pl.when(z > 0)
+        def _():
+            xdn(p).wait_send()
+
+        @pl.when((z == 0) | (z == 3))
+        def _():
+            ysend(blk(q, z, p), z, p).wait_send()
     for p in range(NP):
         @pl.when(z < 3)
         def _():
@@ -572,7 +653,8 @@
             def _():
                 dn(blk(q, z + s, p), z + s, p).wait_send()
         for b in range(SRC):
-            ysend(blk(q, b, p), b, p).wait_send()
+            if p < NP // 2 or b in (1, 2):
+                ysend(blk(q, b, p), b, p).wait_send()
             csend(blk(q, b, p), q, 0, b, p).wait_send()
             csend(blk(qy, b, p), qy, 1, b, p).wait_send()
     for cc in range(last + 1):
@@ -622,6 +704,7 @@
             sem((NA,)), sem((NB, 2)),
             sem((4, NP)), sem((4, NP)), sem((4, NP)),
             sem((4, NP)), sem((4, NP)),
+            sem((NP,)), sem((NP,)), sem((2, NP)),
             sem((2, 4, NP)), sem((2, 4, NP)),
             sem((len(CHUNKS), 3)), sem((len(CHUNKS), 3)),
             sem((len(CHUNKS), 3)), sem((len(CHUNKS), 3)),

time: 119 us -> 111 us (0.933)
  Pallas kernels: 117 us -> 108 us
    pallas_call x1, Pallas kernels: 97.7 us -> 90.3 us  [moe_call(): pl.pallas_call(moe_kernel, out_shape=jax.ShapeDtypeStruct((rows, dm), bf1...]
where the time goes in v3:
time: 111 us; the launch traced here: 110 us
  Pallas kernels  108 us (97%)
  local copies, waits for them, and re-layouts  1.67 us (2%)
    pallas_call x1, Pallas kernels, moe_call(): pl.pallas_call(moe_kernel, out_shape=jax.ShapeDtypeStruct((rows, dm), bf1...  90.3 us
    pallas_call x1, Pallas kernels, attn_call(): pl.pallas_call(attn_kernel, out_shape=(jax.ShapeDtypeStruct((rows, dm + 1...  17.8 us

profile of v3, /device:TPU:0, one launch (start us, length us, event | category | flops | bytes accessed | tf_op | source)
XLA Modules:
  0.0 110.4 jit_solution(3507839216246363638)
XLA Ops:
  0.6 17.8 %attn.1 = (bf16[64,2176]{1,0:T(8,128)(2,1)}, bf16[64,2048]{1,0:T(8,128)(2,1)}, bf16[64,64,512]{2,1,0:T(8,128)(2,1)}, bf16[64,64,64]{2,1,0:T(8,128)(2,1)}) custom-call(s32[64]{0:T(128)} %pos_sm.1, bf16[64,2048]{1,0:T(8,128)(2,1)} %x_ref.1, s32[1,64]{1,0:T(1,128)} %bitcast.9, s32[6,64]{1,0:T(8,128)} %bitcast.8, f32[1,128]{1,0:T(1,128)} %constant.2.clone.freq_ref, ...), custom_call_target="tpu_custom_call" | custom-call | tf_op jit(solution)/shard_map/attn/pallas_call | solution.py:170
  18.4 90.3 %moe.1 = bf16[64,2048]{1,0:T(8,128)(2,1)} custom-call(bf16[64,2176]{1,0:T(8,128)(2,1)} %get-tuple-element.7.hx_ref, bf16[64,2048]{1,0:T(8,128)(2,1)} %get-tuple-element.8.res_ref, bf16[64,2048]{1,0:T(8,128)(2,1)} %bitcast.7, bf16[2048,2816]{1,0:T(8,128)(2,1)} %sg_hbm.1, bf16[2048,2816]{1,0:T(8,128)(2,1)} %su_hbm.1, bf16[2,1408,2048]{2,1,0:T(8,128)(2,1)} %bitcast.5, ...), custom_call_target="tpu_custom_call" | custom-call | tf_op jit(solution)/shard_map/moe/pallas_call | solution.py:684
  108.7 1.7 %copy.24 = bf16[64,2048]{1,0:T(8,128)(2,1)} copy(bf16[64,2048]{1,0:T(8,128)(2,1)} %moe.1) | data formatting | bytes 524288

commit v4 on v3

--- a/solution.py
+++ b/solution.py
@@ -11,6 +11,7 @@
 NORM_EPS = 1e-6
 
 MESH = pl.DeviceIdType.MESH
+LANE = 128
 NE = 4
 CAP = 12
 SRC = 4
@@ -21,6 +22,8 @@
 NB = 2
 WIDE = 512
 NP = 4
+DIRECT = (8, 9)
+SETTLED = 4
 AHEAD = 2
 TG = 16
 
@@ -63,13 +66,13 @@
 
     eye = (iota((rows, rows), 0) == iota((rows, rows), 1)).astype(f32).astype(bf16)
     tri = (iota((rows, rows), 0) <= iota((rows, rows), 1)).astype(f32).astype(bf16)
-    expert = iota((128, rows), 0)
-    per_tok = jnp.zeros((128, rows), f32)
+    expert = iota((LANE, rows), 0)
+    per_tok = jnp.zeros((LANE, rows), f32)
     for k in range(ids_ref.shape[0]):
         per_tok = per_tok + jnp.where(ids_ref[k:k + 1] == expert, 1.0, 0.0)
     code = (per_tok * dot(per_tok.astype(bf16), tri)).astype(bf16)
-    hx_ref[:, :128] = dot_nt(eye, code).astype(bf16)
-    posb[...] = dot_nt(eye, jnp.broadcast_to(posr_ref[...].astype(f32), (128, rows)).astype(bf16))
+    hx_ref[:, :LANE] = dot_nt(eye, code).astype(bf16)
+    posb[...] = dot_nt(eye, jnp.broadcast_to(posr_ref[...].astype(f32), (LANE, rows)).astype(bf16))
     angle = posb[...] * freq_ref[...]
     cos, sin = jnp.cos(angle), jnp.sin(angle)
 
@@ -84,21 +87,21 @@
     swapped = jnp.concatenate([-kr[:, rd // 2:], kr[:, :rd // 2]], axis=1)
     ropen[...] = (kr * cos[:, :rd] + swapped * sin[:, :rd]).astype(bf16).astype(f32)
 
-    lo_half = lax.broadcasted_iota(jnp.int32, (1, 128), 1) < 64
-    lo_quarter = lax.broadcasted_iota(jnp.int32, (1, 128), 1) < rd // 2
+    lo_half = lax.broadcasted_iota(jnp.int32, (1, LANE), 1) < 64
+    lo_quarter = lax.broadcasted_iota(jnp.int32, (1, LANE), 1) < rd // 2
 
     def turn(v):
-        swapped = jnp.where(lo_quarter, -pltpu.roll(v, 128 - rd // 2, 1), pltpu.roll(v, rd // 2, 1))
+        swapped = jnp.where(lo_quarter, -pltpu.roll(v, LANE - rd // 2, 1), pltpu.roll(v, rd // 2, 1))
         return (v * cos + swapped * sin).astype(bf16)
 
     m_copy(1).wait()
     for i in range(pairs):
         q_copy(i).wait()
         qp = dot(abuf[...], wq[i]).astype(bf16)
-        t1 = qp[:, 128:256].astype(f32)
+        t1 = qp[:, LANE:256].astype(f32)
         t2 = pltpu.roll(qp[:, 256:].astype(f32), 64, 1)
         odd = jnp.where(lo_half, pltpu.roll(t1, 64, 1), t2).astype(bf16)
-        qlat[2 * i] = dot(qp[:, :128], wuk[2 * i]).astype(bf16)
+        qlat[2 * i] = dot(qp[:, :LANE], wuk[2 * i]).astype(bf16)
         qlat[2 * i + 1] = dot(odd, wuk[2 * i + 1]).astype(bf16)
         qrope[2 * i] = turn(t1)
         qrope[2 * i + 1] = turn(t2)
@@ -152,7 +155,7 @@
         rw = r.astype(f32)
         tot = tot + jnp.sum(rw * rw, axis=1, keepdims=True)
     scale = lax.rsqrt(tot / dm + NORM_EPS)
-    hx_ref[:, 128:] = (res_ref[...].astype(f32) * scale * fg_ref[...].astype(f32)[None, :]).astype(bf16)
+    hx_ref[:, LANE:] = (res_ref[...].astype(f32) * scale * fg_ref[...].astype(f32)[None, :]).astype(bf16)
     m_copy(6).wait()
     m_copy(7).wait()
 
@@ -163,14 +166,14 @@
     seq, rd = rope_cache.shape[1:]
     bf16, f32 = jnp.bfloat16, jnp.float32
     freq = ROPE_BASE ** (-(2.0 * np.arange(rd // 2)) / rd)
-    freq = np.tile(freq.astype(np.float32), 128 // (rd // 2))[None, :]
+    freq = np.tile(freq.astype(np.float32), LANE // (rd // 2))[None, :]
     vm = pl.BlockSpec(memory_space=pltpu.VMEM)
     hb = pl.BlockSpec(memory_space=pl.ANY)
     pw = 2 * (nope + rd)
     return pl.pallas_call(
         attn_kernel,
         out_shape=(
-            jax.ShapeDtypeStruct((rows, dm + 128), bf16),
+            jax.ShapeDtypeStruct((rows, dm + LANE), bf16),
             jax.ShapeDtypeStruct((rows, dm), bf16),
             jax.ShapeDtypeStruct(lat_cache.shape, bf16),
             jax.ShapeDtypeStruct(rope_cache.shape, bf16),
@@ -189,10 +192,10 @@
             pltpu.VMEM((rows, rank), f32),
             pltpu.VMEM((rows, rd), f32),
             pltpu.VMEM((heads, rows, rank), bf16),
-            pltpu.VMEM((heads, rows, 128), bf16),
+            pltpu.VMEM((heads, rows, LANE), bf16),
             pltpu.VMEM((heads, rows, rank), bf16),
             pltpu.VMEM((rows, heads * nope), bf16),
-            pltpu.VMEM((rows, 128), f32),
+            pltpu.VMEM((rows, LANE), f32),
             pltpu.SemaphoreType.DMA((heads // 2,)),
             pltpu.SemaphoreType.DMA((8,)),
         ],
@@ -254,7 +257,7 @@
     def rcopy(src, dst, ss, rs, d):
         return pltpu.make_async_remote_copy(src_ref=src, dst_ref=dst, send_sem=ss, recv_sem=rs, device_id=d, device_id_type=MESH)
 
-    cut = [0] + [128 + dm * k // NP for k in range(1, NP + 1)]
+    cut = [0] + [LANE + dm * k // NP for k in range(1, NP + 1)]
 
     def part(ref, p):
         return ref.at[:, pl.ds(cut[p], cut[p + 1] - cut[p])]
@@ -263,10 +266,10 @@
         return part(hall.at[qq, b], p)
 
     def up(src, b, p):
-        return rcopy(src, blk(q, b, p), zup_s.at[b, p], z_r.at[b, p], dev(z + 1, q))
+        return rcopy(src, blk(q, b, p), zup_s.at[b], z_r.at[b, p], dev(z + 1, q))
 
     def dn(src, b, p):
-        return rcopy(src, blk(q, b, p), zdn_s.at[b, p], z_r.at[b, p], dev(z - 1, q))
+        return rcopy(src, blk(q, b, p), zdn_s.at[b], z_r.at[b, p], dev(z - 1, q))
 
     def ysend(src, b, p):
         return rcopy(src, blk(q, b, p), y_s.at[b, p], y_r.at[b, p], dev(z, qy))
@@ -275,7 +278,7 @@
         return rcopy(blk(qy, b, p), blk(qy, b, p), y_s.at[b, p], y_r.at[b, p], dev(z, qy))
 
     def csend(src, qq, k, b, p):
-        return rcopy(src, blk(qq, b, p), c_s.at[k, b, p], c_r.at[k, b, p], dev(z, qc))
+        return rcopy(src, blk(qq, b, p), c_s.at[k, b], c_r.at[k, p], dev(z, qc))
 
     for p in range(NP):
         mine = part(hx_ref, p)
@@ -402,7 +405,7 @@
         if part == 0:
             a_copy(2 * j).wait()
             a_copy(2 * j + 1).wait()
-        gate_up(lambda: hx_ref[:, pl.ds(128, dm)], (2 * j) % NA, (2 * j + 1) % NA, sh_put(j), cols[part], cols[part + 1])
+        gate_up(lambda: hx_ref[:, pl.ds(LANE, dm)], (2 * j) % NA, (2 * j + 1) % NA, sh_put(j), cols[part], cols[part + 1])
 
     @fenced
     def sh_down(p):
@@ -448,7 +451,7 @@
         owner = jnp.where(blk == 0, q, jnp.where(blk == 1, qc, jnp.where(blk == 2, qy, qd)))
         rep = (ee == SRC * NE * z + NE * owner + lax.div(lax.rem(col, NE * GRP), GRP)).astype(f32).astype(bf16)
         for b in range(SRC):
-            hz = hall[q, b, :, pl.ds(128, dm)]
+            hz = hall[q, b, :, pl.ds(LANE, dm)]
             code = hall[q, b, :, pl.ds(0, rtr_ref.shape[0])]
             s = jax.nn.sigmoid(lax.dot_general(hz, rtr_ref[...], (((1,), (1,)), ((), ())), preferred_element_type=f32))
             chosen = jnp.where(code.astype(f32) > 0.0, s, 0.0)
@@ -464,15 +467,15 @@
     @fenced
     def find(g):
         nr = NE * GRP
-        ee = lax.broadcasted_iota(jnp.int32, (nr, 128), 1)
-        ri = lax.broadcasted_iota(jnp.int32, (nr, 128), 0)
+        ee = lax.broadcasted_iota(jnp.int32, (nr, LANE), 1)
+        ri = lax.broadcasted_iota(jnp.int32, (nr, LANE), 0)
         lo = (ee - NE * me) * GRP
         sel = ((ri >= lo) & (ri < lo + GRP)).astype(f32).astype(bf16)
         rcol = lax.broadcasted_iota(jnp.int32, (nr, 1), 0)
         r48 = lax.rem(rcol, GRP)
         row_z = lax.div(r48, CAP)
         row_k = (lax.rem(r48, CAP) + 1).astype(f32)
-        code = hall[g, :, :, pl.ds(0, 128)].reshape(SRC * rows, 128)
+        code = hall[g, :, :, pl.ds(0, LANE)].reshape(SRC * rows, LANE)
         ct = lax.dot_general(sel, code, (((1,), (1,)), ((), ())), preferred_element_type=f32)
         tz = lax.div(lax.broadcasted_iota(jnp.int32, (1, SRC * rows), 1), rows)
         pick[g] = jnp.where((ct == row_k) & (row_z == tz), 1.0, 0.0).astype(bf16)
@@ -480,7 +483,7 @@
     @fenced
     def select(g, p):
         wide = dm // NP
-        hz = hall[g, :, :, pl.ds(128 + p * wide, wide)].reshape(SRC * rows, wide)
+        hz = hall[g, :, :, pl.ds(LANE + p * wide, wide)].reshape(SRC * rows, wide)
         x = dot(pick[g], hz).astype(bf16)
         for i in range(NE):
             xbuf[i, g, :, pl.ds(p * wide, wide)] = x[i * GRP:(i + 1) * GRP]
@@ -495,8 +498,8 @@
         if p + 1 < NP:
             gather_step(4, p + 1)
         for k, qq in ((0, qc), (1, qd)):
-            for b in range(SRC):
-                rcopy(blk(qq, b, p), blk(qq, b, p), c_s.at[k, b, p], c_r.at[k, b, p], dev(z, qc)).wait_recv()
+            got = hall.at[qq, :, :, pl.ds(cut[p], cut[p + 1] - cut[p])]
+            rcopy(got, got, c_s.at[k, 0], c_r.at[k, p], dev(z, qc)).wait_recv()
         for qq in peers:
             if p == 0:
                 find(qq)
@@ -520,23 +523,23 @@
 
     def s_copy(cc, j):
         g0, n = CHUNKS[cc]
-        return rcopy(sbuf.at[pl.ds(g0, n), peers[j]], rbuf.at[pl.ds(g0, n), j], s_s.at[cc, j], s_r.at[cc, j], dev(z, peers[j]))
+        return rcopy(sbuf.at[pl.ds(g0, n), peers[j]], rbuf.at[pl.ds(g0, n), j], s_s.at[cc, j], s_r.at[cc], dev(z, peers[j]))
 
     @fenced
     def down(cc):
         g0, n = CHUNKS[cc]
-        w = g0 * 128 // cw
-        off = g0 * 128 % cw
+        w = g0 * LANE // cw
+        off = g0 * LANE % cw
         if off == 0:
             b_copy(w).wait()
         for i in range(NE):
-            o = dot(act[i], bbuf[w % NB, i, :, pl.ds(off, n * 128)]).astype(bf16)
+            o = dot(act[i], bbuf[w % NB, i, :, pl.ds(off, n * LANE)]).astype(bf16)
             for g in range(4):
                 for t in range(n):
-                    sbuf[g0 + t, g, pl.ds(i * GRP, GRP)] = o[g * GRP:(g + 1) * GRP, t * 128:(t + 1) * 128]
+                    sbuf[g0 + t, g, pl.ds(i * GRP, GRP)] = o[g * GRP:(g + 1) * GRP, t * LANE:(t + 1) * LANE]
         for j in (2, 1, 0):
             s_copy(cc, j).start()
-        if off + n * 128 == cw and w + NB < NCH:
+        if off + n * LANE == cw and w + NB < NCH:
             b_copy(w + NB).start()
 
     last = len(CHUNKS) - 1
@@ -548,7 +551,7 @@
 
     def f_copy(cc, dst_z, k, rk):
         g0, n = CHUNKS[cc]
-        return rcopy(fbuf.at[pl.ds(g0, n), dst_z], zbuf.at[pl.ds(g0, n), rk], f_s.at[cc, k], f_r.at[cc, rk], dev(dst_z, q))
+        return rcopy(fbuf.at[pl.ds(g0, n), dst_z], zbuf.at[pl.ds(g0, n), rk], f_s.at[cc, k], f_r.at[cc], dev(dst_z, q))
 
     def l_copy(cc):
         g0, n = CHUNKS[cc]
@@ -557,22 +560,26 @@
     @fenced
     def combine(cc):
         g0, n = CHUNKS[cc]
-        for j in range(3):
-            s_copy(cc, j).wait_recv()
+        rows_in = rbuf.at[pl.ds(g0, n)]
+        rcopy(rows_in, rows_in, s_s.at[cc, 0], s_r.at[cc], dev(z, qc)).wait_recv()
         got = jnp.concatenate([jnp.concatenate([sbuf[g0 + t, q]] + [rbuf[g0 + t, j] for j in range(3)], axis=0) for t in range(n)], axis=1)
         acc = dot(w3[0], got) + (dot(w3[1], got) + dot(w3[2], got))
         for t in range(n):
-            fbuf[g0 + t] = acc[:, t * 128:(t + 1) * 128].reshape(SRC, rows, 128)
+            fbuf[g0 + t] = acc[:, t * LANE:(t + 1) * LANE].reshape(SRC, rows, LANE)
 
         @pl.when(edge)
         def _():
-            l_copy(cc).start()
-            for c in ((cc - 1, cc) if cc == last else (cc,) if cc < last - 1 else ()):
-                f_copy(c, z_mid2, 1, 2).start()
-                f_copy(c, z_mid, 0, 0).start()
+            if cc in DIRECT:
+                f_copy(cc, z_edge2, 2, 2).start()
+            else:
+                l_copy(cc).start()
+            f_copy(cc, z_mid2, 1, 2).start()
+            f_copy(cc, z_mid, 0, 0).start()
 
         @pl.when(jnp.logical_not(edge))
         def _():
+            if cc in DIRECT:
+                f_copy(cc, z_edge2, 2, 1).start()
             f_copy(cc, z_mid2, 1, 1).start()
             f_copy(cc, z_edge, 0, 0).start()
 
@@ -592,23 +599,72 @@
         g0, n = CHUNKS[cc]
 
         def finish(parts):
-            for rk in range(parts):
-                f_copy(cc, z_mid, 0, rk).wait_recv()
+            sums = zbuf.at[pl.ds(g0, n), pl.ds(0, parts)]
+            rcopy(sums, sums, f_s.at[cc, 0], f_r.at[cc], dev(z, qc)).wait_recv()
             for t in range(g0, g0 + n):
-                cols = pl.ds(t * 128, 128)
+                cols = pl.ds(t * LANE, LANE)
                 tot = fbuf[t, z]
                 for rk in range(parts):
                     tot = tot + zbuf[t, rk]
-                sh = sout[t * 128 // cw, :, pl.ds(t * 128 % cw, 128)]
+                sh = sout[t * LANE // cw, :, pl.ds(t * LANE % cw, LANE)]
                 out_ref[:, cols] = (res_ref[:, cols].astype(f32) + sh + tot).astype(bf16)
 
         @pl.when(edge)
         def _():
-            finish(2)
+            finish(3 if cc in DIRECT else 2)
 
         @pl.when(jnp.logical_not(edge))
         def _():
             finish(3)
+
+    @fenced
+    def drain_gather():
+        for p in range(NP // 2, NP):
+            @pl.when(z < 3)
+            def _():
+                xup(p).wait_send()
+
+            @pl.when(z > 0)
+            def _():
+                xdn(p).wait_send()
+
+            @pl.when((z == 0) | (z == 3))
+            def _():
+                ysend(blk(q, z, p), z, p).wait_send()
+        for p in range(NP):
+            for b in range(SRC):
+                if p < NP // 2 or b in (1, 2):
+                    ysend(blk(q, b, p), b, p).wait_send()
+        for b in range(SRC):
+            whole = hall.at[q, b]
+
+            @pl.when((z < 3) & (b <= z))
+            def _():
+                rcopy(whole, whole, zup_s.at[b], z_r.at[b, 0], dev(z + 1, q)).wait_send()
+
+            @pl.when((z > 0) & (b >= z))
+            def _():
+                rcopy(whole, whole, zdn_s.at[b], z_r.at[b, 0], dev(z - 1, q)).wait_send()
+            for k in range(2):
+                rcopy(whole, whole, c_s.at[k, b], c_r.at[k, 0], dev(z, qc)).wait_send()
+
+    @fenced
+    def drain(cc):
+        for j in range(3):
+            s_copy(cc, j).wait_send()
+        f_copy(cc, z_mid, 0, 0).wait_send()
+        f_copy(cc, z_mid, 1, 0).wait_send()
+        if cc in DIRECT:
+            f_copy(cc, z_mid, 2, 0).wait_send()
+            return
+
+        @pl.when(edge)
+        def _():
+            l_copy(cc).wait_send()
+
+        @pl.when(jnp.logical_not(edge))
+        def _():
+            f_copy(cc, z_edge2, 2, 1).wait_send()
 
     for cc in range(AHEAD):
         down(cc)
@@ -616,60 +672,17 @@
     for cc in range(last + 1):
         if cc + AHEAD <= last:
             down(cc + AHEAD)
+        if cc == AHEAD:
+            drain_gather()
+        if cc >= SETTLED:
+            drain(cc - SETTLED)
         combine(cc)
-        if cc:
+        if cc and cc - 1 not in DIRECT:
             relay(cc - 1)
-    relay(last)
     for cc in range(last + 1):
         final(cc)
-
-    for p in range(NP // 2, NP):
-        @pl.when(z < 3)
-        def _():
-            xup(p).wait_send()
-
-        @pl.when(z > 0)
-        def _():
-            xdn(p).wait_send()
-
-        @pl.when((z == 0) | (z == 3))
-        def _():
-            ysend(blk(q, z, p), z, p).wait_send()
-    for p in range(NP):
-        @pl.when(z < 3)
-        def _():
-            up(part(hx_ref, p), z, p).wait_send()
-
-        @pl.when(z > 0)
-        def _():
-            dn(part(hx_ref, p), z, p).wait_send()
-
-        for s in range(1, 4):
-            @pl.when((z - s >= 0) & (z < 3))
-            def _():
-                up(blk(q, z - s, p), z - s, p).wait_send()
-
-            @pl.when((z + s <= 3) & (z > 0))
-            def _():
-                dn(blk(q, z + s, p), z + s, p).wait_send()
-        for b in range(SRC):
-            if p < NP // 2 or b in (1, 2):
-                ysend(blk(q, b, p), b, p).wait_send()
-            csend(blk(q, b, p), q, 0, b, p).wait_send()
-            csend(blk(qy, b, p), qy, 1, b, p).wait_send()
-    for cc in range(last + 1):
-        for j in range(3):
-            s_copy(cc, j).wait_send()
-        f_copy(cc, z_mid, 0, 0).wait_send()
-        f_copy(cc, z_mid, 1, 0).wait_send()
-
-        @pl.when(edge)
-        def _():
-            l_copy(cc).wait_send()
-
-        @pl.when(jnp.logical_not(edge))
-        def _():
-            f_copy(cc, z_edge2, 2, 1).wait_send()
+    for cc in range(last + 1 - SETTLED, last + 1):
+        drain(cc)
 
 
 def moe_call(hx, resid, router, sh_gate, sh_up, sh_down, ex_gate, ex_up, ex_down):
@@ -687,27 +700,27 @@
         in_specs=[vm] * 3 + [hb] * 6,
         out_specs=vm,
         scratch_shapes=[
-            pltpu.VMEM((4, SRC, rows, dm + 128), bf16),
+            pltpu.VMEM((4, SRC, rows, dm + LANE), bf16),
             pltpu.VMEM((NE, 4, GRP, dm), bf16),
             pltpu.VMEM((NE, SRC * GRP, ff), bf16),
             pltpu.VMEM((2, rows, ff), bf16),
             pltpu.VMEM((NCH, rows, cw), f32),
             pltpu.VMEM((NA, dm, ff), bf16),
             pltpu.VMEM((NB, NE, ff, cw), bf16),
-            pltpu.VMEM((dm // 128, 4, nk, 128), bf16),
-            pltpu.VMEM((dm // 128, 3, nk, 128), bf16),
-            pltpu.VMEM((dm // 128, SRC, rows, 128), f32),
-            pltpu.VMEM((dm // 128, 3, rows, 128), f32),
-            pltpu.VMEM((dm // 128, rows, 128), f32),
+            pltpu.VMEM((dm // LANE, 4, nk, LANE), bf16),
+            pltpu.VMEM((dm // LANE, 3, nk, LANE), bf16),
+            pltpu.VMEM((dm // LANE, SRC, rows, LANE), f32),
+            pltpu.VMEM((dm // LANE, 3, rows, LANE), f32),
+            pltpu.VMEM((dm // LANE, rows, LANE), f32),
             pltpu.VMEM((3, SRC * rows, SRC * nk), bf16),
             pltpu.VMEM((4, nk, SRC * rows), bf16),
             sem((NA,)), sem((NB, 2)),
-            sem((4, NP)), sem((4, NP)), sem((4, NP)),
+            sem((4,)), sem((4,)), sem((4, NP)),
             sem((4, NP)), sem((4, NP)),
             sem((NP,)), sem((NP,)), sem((2, NP)),
-            sem((2, 4, NP)), sem((2, 4, NP)),
-            sem((len(CHUNKS), 3)), sem((len(CHUNKS), 3)),
-            sem((len(CHUNKS), 3)), sem((len(CHUNKS), 3)),
+            sem((2, 4)), sem((2, NP)),
+            sem((len(CHUNKS), 3)), sem((len(CHUNKS),)),
+            sem((len(CHUNKS), 3)), sem((len(CHUNKS),)),
             sem((len(CHUNKS),)), sem((len(CHUNKS),)),
         ],
         compiler_params=pltpu.CompilerParams(collective_id=0, has_side_effects=True, vmem_limit_bytes=66 * 1024 * 1024 - 2 * 1024 * 1024 - 65536),

time: 111 us -> 109 us (0.982)
    pallas_call x1, Pallas kernels: 90.3 us -> 89.1 us  [moe_call(): pl.pallas_call(moe_kernel, out_shape=jax.ShapeDtypeStruct((rows, dm), bf1...]
where the time goes in v4:
time: 109 us
  Pallas kernels  107 us (98%)
  local copies, waits for them, and re-layouts  1.67 us (2%)
    pallas_call x1, Pallas kernels, moe_call(): pl.pallas_call(moe_kernel, out_shape=jax.ShapeDtypeStruct((rows, dm), bf1...  89.1 us
    pallas_call x1, Pallas kernels, attn_call(): pl.pallas_call(attn_kernel, out_shape=(jax.ShapeDtypeStruct((rows, dm + L...  17.8 us

profile of v4, /device:TPU:0, one launch (start us, length us, event | category | flops | bytes accessed | tf_op | source)
XLA Modules:
  0.0 109.3 jit_solution(18273148417360218436)
XLA Ops:
  0.6 17.8 %attn.1 = (bf16[64,2176]{1,0:T(8,128)(2,1)}, bf16[64,2048]{1,0:T(8,128)(2,1)}, bf16[64,64,512]{2,1,0:T(8,128)(2,1)}, bf16[64,64,64]{2,1,0:T(8,128)(2,1)}) custom-call(s32[64]{0:T(128)} %pos_sm.1, bf16[64,2048]{1,0:T(8,128)(2,1)} %x_ref.1, s32[1,64]{1,0:T(1,128)} %bitcast.9, s32[6,64]{1,0:T(8,128)} %bitcast.8, f32[1,128]{1,0:T(1,128)} %constant.2.clone.freq_ref, ...), custom_call_target="tpu_custom_call" | custom-call | tf_op jit(solution)/shard_map/attn/pallas_call | solution.py:173
  18.4 89.1 %moe.1 = bf16[64,2048]{1,0:T(8,128)(2,1)} custom-call(bf16[64,2176]{1,0:T(8,128)(2,1)} %get-tuple-element.7.hx_ref, bf16[64,2048]{1,0:T(8,128)(2,1)} %get-tuple-element.8.res_ref, bf16[64,2048]{1,0:T(8,128)(2,1)} %bitcast.7, bf16[2048,2816]{1,0:T(8,128)(2,1)} %sg_hbm.1, bf16[2048,2816]{1,0:T(8,128)(2,1)} %su_hbm.1, bf16[2,1408,2048]{2,1,0:T(8,128)(2,1)} %bitcast.5, ...), custom_call_target="tpu_custom_call" | custom-call | tf_op jit(solution)/shard_map/moe/pallas_call | solution.py:697
  107.6 1.7 %copy.24 = bf16[64,2048]{1,0:T(8,128)(2,1)} copy(bf16[64,2048]{1,0:T(8,128)(2,1)} %moe.1) | data formatting | bytes 524288
